TPU v7x, 128 devices: a whole 4x4x4 slice. The times are simulated.
128 devices in a mesh: gx: 4 (over x), gy: 4 (over z), gz: 8 (over y, core).
Axes of the slice: x: 4, y: 4, z: 4, core: 2. Of those that a mesh axis runs over, the one named last changes fastest.
Arguments:
- right_side: float32 [3, 32, 128, 1024], P(None, 'gx', 'gy', 'gz'), may hold values from -6 to 6
- mass_coef: float32 [3, 32, 128, 1024], P(None, 'gx', 'gy', 'gz'), may hold values from 0.3 to 3
- curl_coef: float32 [3, 32, 128, 1024], P(None, 'gx', 'gy', 'gz'), may hold values from 0.5 to 5
Outputs:
- solution: float32 [3, 32, 128, 1024], P(None, 'gx', 'gy', 'gz')
- residual: float32 [3, 32, 128, 1024], P(None, 'gx', 'gy', 'gz')
All inputs are finite; a program needn't handle non-finite values.
Results may differ from a plain program's by a relative error of at most 0.0003.
Values sent between devices are 32-bit elements; how exact they have to be, the bound alone decides.
No kernel may reach another device: no remote copies, remote signals or barrier semaphores. Data moves between devices by JAX's collectives and lax.ppermute only.
A program may use at most 64 MiB of HBM per device.

v0:
```python
import jax
import jax.numpy as jnp
from jax import lax
from jax.experimental import pallas as pl
from jax.experimental.pallas import tpu as pltpu
from jax.sharding import PartitionSpec as P


HALO = 4
X, Y = 16, 64
OWN = 16
LO, ROWS = 8, 48
WEIGHT = (0.0, 0.5, 0.25, 0.25, 0.25)
VMEM = pl.BlockSpec(memory_space=pltpu.VMEM)


def params(mib):
    return pltpu.CompilerParams(vmem_limit_bytes=mib * 1024 * 1024)


def cost(ns_like):
    return pl.CostEstimate(flops=ns_like, bytes_accessed=1 << 20, transcendentals=0)


def pick(refs, comp):
    return refs[comp // 3], comp % 3


def pack_x(right, mass, curl, low, high):
    refs = (right, mass, curl)
    for comp in range(9):
        ref, c = pick(refs, comp)
        low[comp] = ref[c, 0:4]
        high[comp] = ref[c, 4:8]
    high[4, 0] = mass[1, 4] + curl[2, 3]
    high[5, 0] = mass[2, 4] + curl[1, 3]


def row_tile(refs, below, above, comp, x, y):
    if x < 4:
        return below[comp, x, y : y + 8]
    if x >= 12:
        return above[comp, x - 12, y : y + 8]
    ref, c = pick(refs, comp)
    return ref[c, x - 4, y : y + 8]


def pack_y(right, mass, curl, below, above, low, high):
    refs = (right, mass, curl)
    sub = lax.broadcasted_iota(jnp.int32, (8, 128), 0)
    for comp in range(9):
        for p in range(8):
            a = row_tile(refs, below, above, comp, p, 0)
            b = row_tile(refs, below, above, comp, p + 8, 0)
            low[comp, p] = jnp.where(sub < 4, a, pltpu.roll(b, 4, 0))
            pair = []
            for x in (p, p + 8):
                t = row_tile(refs, below, above, comp, x, 24)
                other = {3: 8, 5: 6}.get(comp)
                if other is not None:
                    t = t + jnp.where(sub == 4, pltpu.roll(row_tile(refs, below, above, other, x, 24), 1, 0), 0.0)
                pair.append(t)
            high[comp, p] = jnp.where(sub < 4, pltpu.roll(pair[0], 4, 0), pair[1])


def halo_tiles(ylow, yhigh, comp, x, sub):
    p = x % 8
    lower, upper = ylow[comp, p], yhigh[comp, p]
    if x < 8:
        lower = pltpu.roll(lower, 4, 0)
    else:
        upper = pltpu.roll(upper, 4, 0)
    return jnp.where(sub >= 4, lower, 0.0), jnp.where(sub < 4, upper, 0.0)


def pack_z(right, mass, curl, below, above, ylow, yhigh, low, high):
    refs = (right, mass, curl)
    sub = lax.broadcasted_iota(jnp.int32, (8, 128), 0)
    lane = lax.broadcasted_iota(jnp.int32, (8, 128), 1)

    def tile(comp, x, o):
        if o == 0:
            return halo_tiles(ylow, yhigh, comp, x, sub)[0]
        if o == 5:
            return halo_tiles(ylow, yhigh, comp, x, sub)[1]
        return row_tile(refs, below, above, comp, x, 8 * (o - 1))

    for comp in range(9):
        other = {3: 7, 4: 6}.get(comp)
        for o in range(6):
            first = jnp.zeros((8, 128), jnp.float32)
            last = first
            for x in range(X):
                t = tile(comp, x, o)
                first = jnp.where((lane // 4) == 2 * x + 1, pltpu.roll(t, 8 * x + 4, 1), first)
                if other is not None:
                    t = t + jnp.where(lane == 124, pltpu.roll(tile(other, x, o), 1, 1), 0.0)
                last = jnp.where((lane // 4) == 2 * x, pltpu.roll(t, (8 * x + 4) % 128, 1), last)
            low[comp, 8 * o : 8 * o + 8] = first
            high[comp, 8 * o : 8 * o + 8] = last


def main(right, mass, curl, below, above, ylow, yhigh, zown_low, zown_high, zlow, zhigh,
         vectors, precond, partial,
         field, coef, diag, node, s, phi, g, fieldS, coefS, diagS, nodeS, sS, phiS, gS):
    f32 = jnp.float32
    sub = lax.broadcasted_iota(jnp.int32, (8, 128), 0)
    lane = lax.broadcasted_iota(jnp.int32, (ROWS, 128), 1)
    first_lane, last_lane = lane == 0, lane == 127

    for comp in range(9):
        ref, c = pick((right, mass, curl), comp)
        to = field.at[0, comp] if comp < 3 else coef.at[comp - 3]
        if comp >= 3:
            to[0] = jnp.zeros((Y, 128), f32)
        to[1:5, OWN : OWN + 32] = below[comp]
        to[5:13, OWN : OWN + 32] = ref[c]
        to[13:17, OWN : OWN + 32] = above[comp]
        for x in range(X):
            lower, upper = halo_tiles(ylow, yhigh, comp, x, sub)
            to[x + 1, OWN - 8 : OWN] = lower
            to[x + 1, OWN + 32 : OWN + 40] = upper
        toS = fieldS.at[0, comp] if comp < 3 else coefS.at[comp - 3]
        toS[0, LO : LO + ROWS] = zown_low[comp] + zlow[comp]
        toS[1, LO : LO + ROWS] = zown_high[comp] + zhigh[comp]

    def at(ref, dy=0):
        return ref[pl.ds(LO + dy, ROWS), :]

    def put(ref, value):
        ref[pl.ds(LO, ROWS), :] = value

    def z_up(value, strip, x):
        return jnp.where(last_lane, pltpu.roll(at(strip), 123 - 8 * x, 1), pltpu.roll(value, 127, 1))

    def z_down(value, strip, x):
        return jnp.where(first_lane, pltpu.roll(at(strip), 125 - 8 * x, 1), pltpu.roll(value, 1, 1))

    def diagonals(m, c, cy, cx, cz, mx, my, mz):
        d0 = m[0] + c[1] + cz[1] + c[2] + cy[2]
        d1 = m[1] + c[2] + cx[2] + c[0] + cz[0]
        d2 = m[2] + c[0] + cy[0] + c[1] + cx[1]
        dn = m[0] + mx + m[1] + my + m[2] + mz
        return 1.0 / d0, 1.0 / d1, 1.0 / d2, 1.0 / dn

    for t in range(2):
        m = [at(coefS.at[c, t]) for c in range(3)]
        c_ = [at(coefS.at[3 + c, t]) for c in range(3)]
        cy = [at(coefS.at[3 + c, t], -1) for c in range(3)]
        cx = [jnp.where(lane < 8, 0.0, pltpu.roll(v, 8, 1)) for v in c_]
        cz = [jnp.where(lane % 8 == 0, 0.0, pltpu.roll(v, 1, 1)) for v in c_]
        out = diagonals(m, c_, cy, cx, cz, pltpu.roll(m[0], 8, 1), at(coefS.at[1, t], -1), pltpu.roll(m[2], 1, 1))
        for c in range(3):
            put(diagS.at[c, t], out[c])
        put(nodeS.at[t], out[3])

    def setup(x, _):
        m = [at(coef.at[c, x + 1]) for c in range(3)]
        c_ = [at(coef.at[3 + c, x + 1]) for c in range(3)]
        cy = [at(coef.at[3 + c, x + 1], -1) for c in range(3)]
        cx = [at(coef.at[3 + c, x]) for c in range(3)]
        cz = [z_down(c_[c], coefS.at[3 + c, 0], x) for c in range(2)]
        out = diagonals(m, c_, cy, cx, cz, at(coef.at[0, x]), at(coef.at[1, x + 1], -1), z_down(m[2], coefS.at[2, 0], x))
        for c in range(3):
            put(diag.at[c, x + 1], out[c])
        put(node.at[x + 1], out[3])
        return 0

    lax.fori_loop(0, X, setup, 0)

    def fluxes(coefs, e, e0y, e0z, e1x, e1z, e2x, e2y):
        return (coefs[0] * ((e2y - e[2]) - (e1z - e[1])),
                coefs[1] * ((e0z - e[0]) - (e2x - e[2])),
                coefs[2] * ((e1x - e[1]) - (e0y - e[0])))

    def curl_back(gv, g0y, g0z, g1x, g1z, g2x, g2y):
        return ((g1z - gv[1]) - (g2y - gv[2]), (g2x - gv[2]) - (g0z - gv[0]), (g0y - gv[0]) - (g1x - gv[1]))

    for k in range(4):
        now, later, before = k % 3, (k + 1) % 3, (k + 2) % 3

        def advance(c, w, r, old):
            v = w - r
            return v if k == 0 else v - WEIGHT[k] * old

        for t in range(2):
            r = [at(fieldS.at[now, c, t]) for c in range(3)]
            q = ((pltpu.roll(r[0], 8, 1) - r[0]) + (at(fieldS.at[now, 1, t], -1) - r[1])) + (pltpu.roll(r[2], 1, 1) - r[2])
            put(phiS.at[t], q * at(nodeS.at[t]))
            for c in range(3):
                put(sS.at[c, t], r[c] * at(diagS.at[c, t]))
        for t in range(2):
            e = [at(sS.at[c, t]) for c in range(3)]
            out = fluxes([at(coefS.at[3 + c, t]) for c in range(3)], e,
                         at(sS.at[0, t], 1), pltpu.roll(e[0], 127, 1), pltpu.roll(e[1], 120, 1),
                         pltpu.roll(e[1], 127, 1), pltpu.roll(e[2], 120, 1), at(sS.at[2, t], 1))
            for c in range(3):
                put(gS.at[c, t], out[c])

        def first(x, _):
            r = [at(field.at[now, c, x + 1]) for c in range(3)]
            q = ((at(field.at[now, 0, x]) - r[0]) + (at(field.at[now, 1, x + 1], -1) - r[1])) + (
                z_down(r[2], fieldS.at[now, 2, 0], x) - r[2])
            put(phi.at[x + 1], q * at(node.at[x + 1]))
            for c in range(3):
                put(s.at[c, x + 1], r[c] * at(diag.at[c, x + 1]))
            return 0

        lax.fori_loop(k, 16 - k, first, 0)

        def second(x, _):
            e = [at(s.at[c, x + 1]) for c in range(3)]
            out = fluxes([at(coef.at[3 + c, x + 1]) for c in range(3)], e,
                         at(s.at[0, x + 1], 1), z_up(e[0], sS.at[0, 1], x), at(s.at[1, x + 2]),
                         z_up(e[1], sS.at[1, 1], x), at(s.at[2, x + 2]), at(s.at[2, x + 1], 1))
            for c in range(3):
                put(g.at[c, x + 1], out[c])
            return 0

        lax.fori_loop(k, 15 - k, second, 0)

        def third(x, own, sums):
            gv = [at(g.at[c, x + 1]) for c in range(3)]
            w = curl_back(gv, at(g.at[0, x + 1], -1), z_down(gv[0], gS.at[0, 0], x), at(g.at[1, x]),
                          z_down(gv[1], gS.at[1, 0], x), at(g.at[2, x]), at(g.at[2, x + 1], -1))
            p = at(phi.at[x + 1])
            up = (at(phi.at[x + 2]), at(phi.at[x + 1], 1), z_up(p, phiS.at[1], x))
            for c in range(3):
                u = at(s.at[c, x + 1]) + (up[c] - p)
                r = at(field.at[now, c, x + 1])
                old = None if k == 0 else at(field.at[before, c, x + 1])
                v = advance(c, w[c] + at(coef.at[c, x + 1]) * u, r, old)
                put(field.at[later, c, x + 1], v)
                if own:
                    u, r, v = (a[OWN - LO : OWN - LO + 32] for a in (u, r, v))
                    vectors[k, c, x - 4] = v
                    precond[k, c, x - 4] = u
                    ru, vu = r * u, v * u
                    sums = (sums[0] + ((ru[0:8] + ru[8:16]) + (ru[16:24] + ru[24:32])),
                            sums[1] + ((vu[0:8] + vu[8:16]) + (vu[16:24] + vu[24:32])))
            return sums

        def outside(x, carry):
            third(x, False, None)
            return carry

        zero = jnp.zeros((8, 128), f32)
        lax.fori_loop(k + 1, 4, outside, 0)
        sums = lax.fori_loop(4, 12, lambda x, carry: third(x, True, carry), (zero, zero))
        lax.fori_loop(12, 15 - k, outside, 0)
        for i in range(2):
            partial[2 * k + i] = sums[i]

        if k < 3:
            for t in range(2):
                gv = [at(gS.at[c, t]) for c in range(3)]
                w = curl_back(gv, at(gS.at[0, t], -1), pltpu.roll(gv[0], 1, 1), pltpu.roll(gv[1], 8, 1),
                              pltpu.roll(gv[1], 1, 1), pltpu.roll(gv[2], 8, 1), at(gS.at[2, t], -1))
                p = at(phiS.at[t])
                up = (pltpu.roll(p, 120, 1), at(phiS.at[t], 1), pltpu.roll(p, 127, 1))
                for c in range(3):
                    u = at(sS.at[c, t]) + (up[c] - p)
                    old = None if k == 0 else at(fieldS.at[before, c, t])
                    put(fieldS.at[later, c, t],
                        advance(c, w[c] + at(coefS.at[c, t]) * u, at(fieldS.at[now, c, t]), old))


def fold(partial, out):
    lane = lax.broadcasted_iota(jnp.int32, (1, 128), 1)
    row = jnp.zeros((1, 128), jnp.float32)
    for d in range(8):
        t = jnp.sum(partial[d], axis=0, keepdims=True)
        for shift in (64, 32, 16):
            t = t + pltpu.roll(t, shift, 1)
        row = jnp.where(lane // 16 == d, t, row)
    out[...] = jnp.broadcast_to(row, out.shape)


def finish(everyone, right, vectors, precond, solution_out, residual_out):
    total = jnp.sum(everyone[...], axis=0, keepdims=True)
    lane = lax.broadcasted_iota(jnp.int32, (1, 128), 1)
    dots = [jnp.broadcast_to(jnp.sum(jnp.where(lane // 16 == d, total, 0.0), axis=1, keepdims=True), (8, 128))
            for d in range(8)]
    size = [1.0] + [2.0 ** (1 - k) for k in range(1, 9)]
    moment = [dots[0], dots[1]]
    for k in range(1, 4):
        moment.append((dots[2 * k] * (2.0 / size[k] ** 2) - moment[0]) * size[2 * k])
        moment.append((dots[2 * k + 1] * (2.0 / (size[k] * size[k + 1])) - moment[1]) * size[2 * k + 1])
    row, earlier = moment, None
    alpha, beta = [row[1] / row[0]], [None]
    for k in range(1, 4):
        following = [None] * 8
        for l in range(k, 8 - k):
            t = row[l + 1] - alpha[k - 1] * row[l] + WEIGHT[l if l < 2 else 2] * row[l - 1]
            if k > 1:
                t = t - beta[k - 1] * earlier[l]
            following[l] = t
        alpha.append(following[k + 1] / following[k] - row[k] / row[k - 1])
        beta.append(following[k] / row[k - 1])
        row, earlier = following, row
    zero = jnp.zeros((8, 128), jnp.float32)
    older, newer = [zero] * 6, [zero + 1.0] + [zero] * 5
    value_older, value = zero, zero + 1.0
    weight = lambda l: WEIGHT[min(l, 2)]
    for k in range(4):
        nxt = []
        for l in range(6):
            t = -alpha[k] * newer[l]
            if l > 0:
                t = t + newer[l - 1]
            if l < 5:
                t = t + weight(l + 1) * newer[l + 1]
            if k > 0:
                t = t - beta[k] * older[l]
            nxt.append(t)
        step = (-1.0 - alpha[k]) * value
        if k > 0:
            step = step - beta[k] * value_older
        older, newer, value_older, value = newer, nxt, value, step
    inverse = 1.0 / value
    e = [newer[l] * inverse for l in range(5)]
    S = [None] * 4
    S[3] = -e[4]
    S[2] = -e[3] - S[3]
    S[1] = -e[2] - S[2] - weight(3) * S[3]
    S[0] = -e[1] - S[1] - weight(2) * S[2]
    e = [v[0:1] for v in e]
    S = [v[0:1] for v in S]

    def combine(x, _):
        for c in range(3):
            residual_out[c, x] = (e[0] * right[c, x] + e[1] * vectors[0, c, x]) + (
                e[2] * vectors[1, c, x] + e[3] * vectors[2, c, x]) + e[4] * vectors[3, c, x]
            solution_out[c, x] = (S[0] * precond[0, c, x] + S[1] * precond[1, c, x]) + (
                S[2] * precond[2, c, x] + S[3] * precond[3, c, x])
        return 0

    lax.fori_loop(0, 8, combine, 0)


def shape(*dims):
    return jax.ShapeDtypeStruct(dims, jnp.float32)


def call(kernel, outs, ins, mib, scratch=(), flops=1000000):
    return pl.pallas_call(
        kernel, out_shape=outs, in_specs=[VMEM] * len(ins), out_specs=jax.tree.map(lambda _: VMEM, outs),
        scratch_shapes=list(scratch), compiler_params=params(mib), cost_estimate=cost(flops))(*ins)


def exchange(low, high, axis):
    n = lax.axis_size(axis)
    up = [(i, (i + 1) % n) for i in range(n)]
    return lax.ppermute(high, axis, up), lax.ppermute(low, axis, [(j, i) for i, j in up])


def body(right, mass, curl):
    args = (right, mass, curl)
    low, high = call(pack_x, (shape(9, 4, 32, 128),) * 2, args, 8)
    args += exchange(low, high, "gx")
    low, high = call(pack_y, (shape(9, 8, 8, 128),) * 2, args, 12)
    args += exchange(low, high, "gy")
    low, high = call(pack_z, (shape(9, ROWS, 128),) * 2, args, 16)
    args += (low, high) + exchange(low, high, "gz")
    V = pltpu.VMEM
    f32 = jnp.float32
    vectors, precond, partial = call(
        main, (shape(4, 3, 8, 32, 128), shape(4, 3, 8, 32, 128), shape(8, 8, 128)), args, 46,
        [V((3, 3, 18, Y, 128), f32), V((6, 18, Y, 128), f32), V((3, 18, Y, 128), f32), V((18, Y, 128), f32),
         V((3, 18, Y, 128), f32), V((18, Y, 128), f32), V((3, 18, Y, 128), f32),
         V((3, 3, 2, Y, 128), f32), V((6, 2, Y, 128), f32), V((3, 2, Y, 128), f32), V((2, Y, 128), f32),
         V((3, 2, Y, 128), f32), V((2, Y, 128), f32), V((3, 2, Y, 128), f32)])
    axes = ("gx", "gy", "gz")
    devices = lax.axis_size(axes)
    (rows,) = call(fold, (shape(devices, 128),), (partial,), 4)
    everyone = lax.all_to_all(rows.reshape(devices, 1, 128), axes, 0, 0, tiled=True).reshape(devices, 128)
    return call(finish, (shape(3, 8, 32, 128),) * 2, (everyone, right, vectors, precond), 16)


def solution(mesh):
    spec = P(None, "gx", "gy", "gz")
    return jax.shard_map(body, mesh=mesh, in_specs=(spec,) * 3, out_specs=(spec,) * 2, check_vma=False)
```

profile of v0, /device:TPU:1, one launch (start us, length us, event | category | flops | bytes accessed | tf_op | source)
XLA Modules:
  0.0 91.0 jit_solution(7567303484145339871)
XLA Ops:
  0.6 0.0 copy-start
  0.6 1.0 %copy-done = f32[3,8,32,128]{3,2,1,0:T(8,128)S(1)} copy-done((f32[3,8,32,128]{3,2,1,0:T(8,128)S(1)}, f32[3,8,32,128]{3,2,1,0:T(8,128)}, u32[]{:S(2)}) %copy-start) | copy-done | bytes 393240
  1.6 1.0 %copy-done.3 = f32[3,8,32,128]{3,2,1,0:T(8,128)S(1)} copy-done((f32[3,8,32,128]{3,2,1,0:T(8,128)S(1)}, f32[3,8,32,128]{3,2,1,0:T(8,128)}, u32[]{:S(2)}) %copy-start.3) | copy-done | bytes 393240
  2.6 1.0 %copy-done.6 = f32[3,8,32,128]{3,2,1,0:T(8,128)S(1)} copy-done((f32[3,8,32,128]{3,2,1,0:T(8,128)S(1)}, f32[3,8,32,128]{3,2,1,0:T(8,128)}, u32[]{:S(2)}) %copy-start.6) | copy-done | bytes 393240
  3.6 0.1 shard_map.50
  3.7 2.1 %collective-permute-start = (f32[9,4,32,128]{3,2,1,0:T(8,128)S(1)}, f32[9,4,32,128]{3,2,1,0:T(8,128)S(1)}, u32[]{:S(2)}, u32[]{:S(2)}) collective-permute-start(f32[9,4,32,128]{3,2,1,0:T(8,128)S(1)} %get-tuple-element.11), channel_id=1, source_target_pairs={{0,32},{32,64},{64,96},{96,0},{1,33},{33,65},{65,97},{97,1},{2,34}... | collective-permute-start | bytes 1769480 | tf_op jit(solution)/shard_map/ppermute | solution.py:354
  5.8 1.3 %collective-permute-start.1 = (f32[9,4,32,128]{3,2,1,0:T(8,128)S(1)}, f32[9,4,32,128]{3,2,1,0:T(8,128)S(1)}, u32[]{:S(2)}, u32[]{:S(2)}) collective-permute-start(f32[9,4,32,128]{3,2,1,0:T(8,128)S(1)} %get-tuple-element.12), channel_id=1, source_target_pairs={{32,0},{64,32},{96,64},{0,96},{33,1},{65,33},{97,65},{1,97},{34,2}... | collective-permute-start | bytes 1769480 | tf_op jit(solution)/shard_map/ppermute | solution.py:354
  7.2 12.6 %collective-permute-done.below = f32[9,4,32,128]{3,2,1,0:T(8,128)S(1)} collective-permute-done((f32[9,4,32,128]{3,2,1,0:T(8,128)S(1)}, f32[9,4,32,128]{3,2,1,0:T(8,128)S(1)}, u32[]{:S(2)}, u32[]{:S(2)}) %collective-permute-start) | collective-permute-done | bytes 589856 | tf_op jit(solution)/shard_map/ppermute | solution.py:354
  19.7 0.0 collective-permute-done.1.above
  19.7 1.0 %copy-done.1 = f32[3,8,32,128]{3,2,1,0:T(8,128)S(1)} copy-done((f32[3,8,32,128]{3,2,1,0:T(8,128)S(1)}, f32[3,8,32,128]{3,2,1,0:T(8,128)}, u32[]{:S(2)}) %copy-start.1) | copy-done | bytes 393240
  20.7 1.0 %copy-done.4 = f32[3,8,32,128]{3,2,1,0:T(8,128)S(1)} copy-done((f32[3,8,32,128]{3,2,1,0:T(8,128)S(1)}, f32[3,8,32,128]{3,2,1,0:T(8,128)}, u32[]{:S(2)}) %copy-start.4) | copy-done | bytes 393240
  21.7 1.0 %copy-done.7 = f32[3,8,32,128]{3,2,1,0:T(8,128)S(1)} copy-done((f32[3,8,32,128]{3,2,1,0:T(8,128)S(1)}, f32[3,8,32,128]{3,2,1,0:T(8,128)}, u32[]{:S(2)}) %copy-start.7) | copy-done | bytes 393240
  22.7 0.1 shard_map.51
  22.8 2.0 %collective-permute-start.2 = (f32[9,8,8,128]{3,2,1,0:T(8,128)S(1)}, f32[9,8,8,128]{3,2,1,0:T(8,128)S(1)}, u32[]{:S(2)}, u32[]{:S(2)}) collective-permute-start(f32[9,8,8,128]{3,2,1,0:T(8,128)S(1)} %get-tuple-element.13), channel_id=1, source_target_pairs={{0,8},{8,16},{16,24},{24,0},{1,9},{9,17},{17,25},{25,1},{2,10},{10... | collective-permute-start | bytes 884744 | tf_op jit(solution)/shard_map/ppermute | solution.py:354
  24.8 2.2 %collective-permute-start.3 = (f32[9,8,8,128]{3,2,1,0:T(8,128)S(1)}, f32[9,8,8,128]{3,2,1,0:T(8,128)S(1)}, u32[]{:S(2)}, u32[]{:S(2)}) collective-permute-start(f32[9,8,8,128]{3,2,1,0:T(8,128)S(1)} %get-tuple-element.14), channel_id=1, source_target_pairs={{8,0},{16,8},{24,16},{0,24},{9,1},{17,9},{25,17},{1,25},{10,2},{18... | collective-permute-start | bytes 884744 | tf_op jit(solution)/shard_map/ppermute | solution.py:354
  27.0 5.8 %collective-permute-done.2.ylow = f32[9,8,8,128]{3,2,1,0:T(8,128)S(1)} collective-permute-done((f32[9,8,8,128]{3,2,1,0:T(8,128)S(1)}, f32[9,8,8,128]{3,2,1,0:T(8,128)S(1)}, u32[]{:S(2)}, u32[]{:S(2)}) %collective-permute-start.2) | collective-permute-done | bytes 294944 | tf_op jit(solution)/shard_map/ppermute | solution.py:354
  32.8 14.4 %shard_map.52 = (f32[9,48,128]{2,1,0:T(8,128)S(1)}, f32[9,48,128]{2,1,0:T(8,128)S(1)}) custom-call(f32[3,8,32,128]{3,2,1,0:T(8,128)S(1)} %copy-done.2, f32[3,8,32,128]{3,2,1,0:T(8,128)S(1)} %copy-done.5, f32[3,8,32,128]{3,2,1,0:T(8,128)S(1)} %copy-done.8, f32[9,4,32,128]{3,2,1,0:T(8,128)S(1)} %collective-permute-done.below, ...), custom_call_target="tpu_custom_call" | custom-call | flops 1000000 | bytes 1048576 | tf_op jit(solution)/shard_map/pallas_call | solution.py:346
  47.2 2.1 %collective-permute-start.5 = (f32[9,48,128]{2,1,0:T(8,128)S(1)}, f32[9,48,128]{2,1,0:T(8,128)S(1)}, u32[]{:S(2)}, u32[]{:S(2)}) collective-permute-start(f32[9,48,128]{2,1,0:T(8,128)S(1)} %get-tuple-element.15.zown_low), channel_id=1, source_target_pairs={{1,0},{2,1},{3,2},{4,3},{5,4},{6,5},{7,6},{0,7},{9,8},{10,9},{11,1... | collective-permute-start | bytes 663560 | tf_op jit(solution)/shard_map/ppermute | solution.py:354
  49.3 1.2 %collective-permute-start.4 = (f32[9,48,128]{2,1,0:T(8,128)S(1)}, f32[9,48,128]{2,1,0:T(8,128)S(1)}, u32[]{:S(2)}, u32[]{:S(2)}) collective-permute-start(f32[9,48,128]{2,1,0:T(8,128)S(1)} %get-tuple-element.16.zown_high), channel_id=1, source_target_pairs={{0,1},{1,2},{2,3},{3,4},{4,5},{5,6},{6,7},{7,0},{8,9},{9,10},{10,1... | collective-permute-start | bytes 663560 | tf_op jit(solution)/shard_map/ppermute | solution.py:354
  50.6 3.9 %collective-permute-done.5.zhigh = f32[9,48,128]{2,1,0:T(8,128)S(1)} collective-permute-done((f32[9,48,128]{2,1,0:T(8,128)S(1)}, f32[9,48,128]{2,1,0:T(8,128)S(1)}, u32[]{:S(2)}, u32[]{:S(2)}) %collective-permute-start.5) | collective-permute-done | bytes 221216 | tf_op jit(solution)/shard_map/ppermute | solution.py:354
  54.4 16.8 %shard_map.53 = (f32[4,3,8,32,128]{4,3,2,1,0:T(8,128)S(1)}, f32[4,3,8,32,128]{4,3,2,1,0:T(8,128)S(1)}, f32[8,8,128]{2,1,0:T(8,128)S(1)}) custom-call(f32[3,8,32,128]{3,2,1,0:T(8,128)S(1)} %copy-done.2, f32[3,8,32,128]{3,2,1,0:T(8,128)S(1)} %copy-done.5, f32[3,8,32,128]{3,2,1,0:T(8,128)S(1)} %copy-done.8, f32[9,4,32,128]{3,2,1,0:T(8,128)S(1)} %collective-permute-done.below, ...), custom_call_target="tpu_custom_call" | custom-call | flops 1000000 | bytes 1048576 | tf_op jit(solution)/shard_map/pallas_call | solution.py:346
  71.3 0.2 shard_map.54
  71.5 18.2 %all_to_all.5 = f32[128,1,128]{2,1,0:T(1,128)S(1)} all-to-all(f32[128,1,128]{2,1,0:T(1,128)S(1)} %bitcast.5), channel_id=1, replica_groups=mesh['gx'=4,'gy'=4,'gz'=8] {'gx','gy','gz'}, dimensions={0} | all-to-all | bytes 131072 | tf_op jit(solution)/shard_map/all_to_all | solution.py:376
  89.8 1.3 %shard_map.55 = (f32[3,8,32,128]{3,2,1,0:T(8,128)}, f32[3,8,32,128]{3,2,1,0:T(8,128)}) custom-call(f32[128,128]{1,0:T(8,128)S(1)} %bitcast.4, f32[3,8,32,128]{3,2,1,0:T(8,128)S(1)} %copy-done.2, f32[4,3,8,32,128]{4,3,2,1,0:T(8,128)S(1)} %get-tuple-element.18.vectors, f32[4,3,8,32,128]{4,3,2,1,0:T(8,128)S(1)} %get-tuple-element.19.precond), custom_call_target="tpu_custom_call" | custom-call | flops 1000000 | bytes 1048576 | tf_op jit(solution)/shard_map/pallas_call | solution.py:346
  (13 shorter events, 0.0 us)
Async XLA Ops:
  0.6 1.0 %copy-start = (f32[3,8,32,128]{3,2,1,0:T(8,128)S(1)}, f32[3,8,32,128]{3,2,1,0:T(8,128)}, u32[]{:S(2)}) copy-start(f32[3,8,32,128]{3,2,1,0:T(8,128)} %right.9) | copy-start | bytes 1179652
  1.6 1.0 %copy-start.3 = (f32[3,8,32,128]{3,2,1,0:T(8,128)S(1)}, f32[3,8,32,128]{3,2,1,0:T(8,128)}, u32[]{:S(2)}) copy-start(f32[3,8,32,128]{3,2,1,0:T(8,128)} %mass.7) | copy-start | bytes 1179652
  2.6 1.0 %copy-start.6 = (f32[3,8,32,128]{3,2,1,0:T(8,128)S(1)}, f32[3,8,32,128]{3,2,1,0:T(8,128)}, u32[]{:S(2)}) copy-start(f32[3,8,32,128]{3,2,1,0:T(8,128)} %curl.7) | copy-start | bytes 1179652
  3.6 29.2 %copy-start.2 = (f32[3,8,32,128]{3,2,1,0:T(8,128)S(1)}, f32[3,8,32,128]{3,2,1,0:T(8,128)}, u32[]{:S(2)}) copy-start(f32[3,8,32,128]{3,2,1,0:T(8,128)} %right.9) | copy-start | bytes 1179652
  3.6 29.2 %copy-start.5 = (f32[3,8,32,128]{3,2,1,0:T(8,128)S(1)}, f32[3,8,32,128]{3,2,1,0:T(8,128)}, u32[]{:S(2)}) copy-start(f32[3,8,32,128]{3,2,1,0:T(8,128)} %mass.7) | copy-start | bytes 1179652
  3.6 29.2 %copy-start.8 = (f32[3,8,32,128]{3,2,1,0:T(8,128)S(1)}, f32[3,8,32,128]{3,2,1,0:T(8,128)}, u32[]{:S(2)}) copy-start(f32[3,8,32,128]{3,2,1,0:T(8,128)} %curl.7) | copy-start | bytes 1179652
  3.7 16.0 %collective-permute-start = (f32[9,4,32,128]{3,2,1,0:T(8,128)S(1)}, f32[9,4,32,128]{3,2,1,0:T(8,128)S(1)}, u32[]{:S(2)}, u32[]{:S(2)}) collective-permute-start(f32[9,4,32,128]{3,2,1,0:T(8,128)S(1)} %get-tuple-element.11), channel_id=1, source_target_pairs={{0,32},{32,64},{64,96},{96,0},{1,33},{33,65},{65,97},{97,1},{2,34}... | collective-permute-start | bytes 1769480 | tf_op jit(solution)/shard_map/ppermute | solution.py:354
  5.8 13.9 %collective-permute-start.1 = (f32[9,4,32,128]{3,2,1,0:T(8,128)S(1)}, f32[9,4,32,128]{3,2,1,0:T(8,128)S(1)}, u32[]{:S(2)}, u32[]{:S(2)}) collective-permute-start(f32[9,4,32,128]{3,2,1,0:T(8,128)S(1)} %get-tuple-element.12), channel_id=1, source_target_pairs={{32,0},{64,32},{96,64},{0,96},{33,1},{65,33},{97,65},{1,97},{34,2}... | collective-permute-start | bytes 1769480 | tf_op jit(solution)/shard_map/ppermute | solution.py:354
  19.7 1.0 %copy-start.1 = (f32[3,8,32,128]{3,2,1,0:T(8,128)S(1)}, f32[3,8,32,128]{3,2,1,0:T(8,128)}, u32[]{:S(2)}) copy-start(f32[3,8,32,128]{3,2,1,0:T(8,128)} %right.9) | copy-start | bytes 1179652
  20.7 1.0 %copy-start.4 = (f32[3,8,32,128]{3,2,1,0:T(8,128)S(1)}, f32[3,8,32,128]{3,2,1,0:T(8,128)}, u32[]{:S(2)}) copy-start(f32[3,8,32,128]{3,2,1,0:T(8,128)} %mass.7) | copy-start | bytes 1179652
  21.7 1.0 %copy-start.7 = (f32[3,8,32,128]{3,2,1,0:T(8,128)S(1)}, f32[3,8,32,128]{3,2,1,0:T(8,128)}, u32[]{:S(2)}) copy-start(f32[3,8,32,128]{3,2,1,0:T(8,128)} %curl.7) | copy-start | bytes 1179652
  22.8 10.0 %collective-permute-start.2 = (f32[9,8,8,128]{3,2,1,0:T(8,128)S(1)}, f32[9,8,8,128]{3,2,1,0:T(8,128)S(1)}, u32[]{:S(2)}, u32[]{:S(2)}) collective-permute-start(f32[9,8,8,128]{3,2,1,0:T(8,128)S(1)} %get-tuple-element.13), channel_id=1, source_target_pairs={{0,8},{8,16},{16,24},{24,0},{1,9},{9,17},{17,25},{25,1},{2,10},{10... | collective-permute-start | bytes 884744 | tf_op jit(solution)/shard_map/ppermute | solution.py:354
  24.8 8.0 %collective-permute-start.3 = (f32[9,8,8,128]{3,2,1,0:T(8,128)S(1)}, f32[9,8,8,128]{3,2,1,0:T(8,128)S(1)}, u32[]{:S(2)}, u32[]{:S(2)}) collective-permute-start(f32[9,8,8,128]{3,2,1,0:T(8,128)S(1)} %get-tuple-element.14), channel_id=1, source_target_pairs={{8,0},{16,8},{24,16},{0,24},{9,1},{17,9},{25,17},{1,25},{10,2},{18... | collective-permute-start | bytes 884744 | tf_op jit(solution)/shard_map/ppermute | solution.py:354
  47.2 7.2 %collective-permute-start.5 = (f32[9,48,128]{2,1,0:T(8,128)S(1)}, f32[9,48,128]{2,1,0:T(8,128)S(1)}, u32[]{:S(2)}, u32[]{:S(2)}) collective-permute-start(f32[9,48,128]{2,1,0:T(8,128)S(1)} %get-tuple-element.15.zown_low), channel_id=1, source_target_pairs={{1,0},{2,1},{3,2},{4,3},{5,4},{6,5},{7,6},{0,7},{9,8},{10,9},{11,1... | collective-permute-start | bytes 663560 | tf_op jit(solution)/shard_map/ppermute | solution.py:354
  49.3 5.1 %collective-permute-start.4 = (f32[9,48,128]{2,1,0:T(8,128)S(1)}, f32[9,48,128]{2,1,0:T(8,128)S(1)}, u32[]{:S(2)}, u32[]{:S(2)}) collective-permute-start(f32[9,48,128]{2,1,0:T(8,128)S(1)} %get-tuple-element.16.zown_high), channel_id=1, source_target_pairs={{0,1},{1,2},{2,3},{3,4},{4,5},{5,6},{6,7},{7,0},{8,9},{9,10},{10,1... | collective-permute-start | bytes 663560 | tf_op jit(solution)/shard_map/ppermute | solution.py:354
where the time goes:
time: 91.4 us; the launch traced here: 91 us
  Pallas kernels  32.9 us (36%)
  waiting for transfers between devices  22.3 us (24%)
  blocking collectives  18.2 us (20%)
  starting transfers between devices  11 us (12%)
  local copies, waits for them, and re-layouts  5.98 us (7%)
    pallas_call x6, Pallas kernels, call(): pl.pallas_call(kernel, out_shape=outs, in_specs=[VMEM] * len(ins), out_sp...  32.9 us
    ppermute x3, waiting for transfers between devices, exchange(): lax.ppermute(high, axis, up)  18.4 us
    all_to_all x1, blocking collectives, body(): lax.all_to_all(rows.reshape(devices, 1, 128), axes, 0, 0, tiled=True)  18.2 us
    unnamed x18, local copies, waits for them, and re-layouts  5.98 us
    ppermute x3, starting transfers between devices, exchange(): lax.ppermute(low, axis, [(j, i) for i, j in up])  5.67 us
    ppermute x3, starting transfers between devices, exchange(): lax.ppermute(high, axis, up)  5.28 us
    ppermute x3, waiting for transfers between devices, exchange(): lax.ppermute(low, axis, [(j, i) for i, j in up])  3.89 us
  transfers between devices with their start and end apart: 6, of which 3 were waited for; matrix products, arithmetic and copies ran while one was open for 0% of the time, Pallas kernels for 0%

commit v1 on v0

v1 whole, which is shorter than its diff:
```python
import jax
import jax.numpy as jnp
from jax import lax
from jax.experimental import pallas as pl
from jax.experimental.pallas import tpu as pltpu
from jax.sharding import PartitionSpec as P


X, Y = 24, 64
OFF, OWN = 4, 16
LO, ROWS = 8, 48
WEIGHT = (0.0, 0.5, 0.25, 0.25, 0.25)
VMEM = pl.BlockSpec(memory_space=pltpu.VMEM)


def load(source, own, low, high):
    def move(c, _):
        for to, x in ((low, 0), (high, 4)):
            value = source[c, x : x + 4]
            own[c, x : x + 4] = value
            to[c] = value
        return 0

    lax.fori_loop(0, 3, move, 0)


def load_mass(source, curl, own, low, high):
    load(source, own, low, high)
    high[1, 0] = source[1, 4] + curl[2, 3]
    high[2, 0] = source[2, 4] + curl[1, 3]


def row_tile(parts, c, x, y):
    own, below, above = parts
    if x < 4:
        return below[c, x, y : y + 8]
    if x >= 12:
        return above[c, x - 12, y : y + 8]
    return own[c, x - 4, y : y + 8]


def pack_y(*refs):
    blocks, (low, high) = (refs[0:3], refs[3:6], refs[6:9]), refs[9:]
    sub = lax.broadcasted_iota(jnp.int32, (8, 128), 0)

    def pack(c, _):
        for n, parts in enumerate(blocks):
            for p in range(8):
                a = row_tile(parts, c, p, 0)
                b = row_tile(parts, c, p + 8, 0)
                low[3 * n + c, p] = jnp.where(sub < 4, a, pltpu.roll(b, 4, 0))
                a = row_tile(parts, c, p, 24)
                b = row_tile(parts, c, p + 8, 24)
                high[3 * n + c, p] = jnp.where(sub < 4, pltpu.roll(a, 4, 0), b)
        return 0

    lax.fori_loop(0, 3, pack, 0)

    def corrected(i, _):
        c, other = 2 * i, 2 - 2 * i
        for p in range(8):
            a = pltpu.roll(row_tile(blocks[2], other, p, 24), 5, 0)
            b = pltpu.roll(row_tile(blocks[2], other, p + 8, 24), 1, 0)
            high[3 + c, p] = high[3 + c, p] + jnp.where(sub == 0, a, jnp.where(sub == 4, b, 0.0))
        return 0

    lax.fori_loop(0, 2, corrected, 0)


def pack_z(*refs):
    blocks, (ylow, yhigh, low, high, field, coef) = (refs[0:3], refs[3:6], refs[6:9]), refs[9:]
    f32 = jnp.float32
    sub = lax.broadcasted_iota(jnp.int32, (8, 128), 0)

    def assemble(c, _):
        for n, (own, below, above) in enumerate(blocks):
            to = field.at[c] if n == 0 else coef.at[3 * n - 3 + c]
            if n > 0:
                to[OFF - 1] = jnp.zeros((Y, 128), f32)
            to[OFF : OFF + 4, OWN : OWN + 32] = below[c]
            to[OFF + 4 : OFF + 12, OWN : OWN + 32] = own[c]
            to[OFF + 12 : OFF + 16, OWN : OWN + 32] = above[c]
            for p in range(8):
                lower, upper = ylow[3 * n + c, p], yhigh[3 * n + c, p]
                to[OFF + p, OWN - 8 : OWN] = jnp.where(sub >= 4, pltpu.roll(lower, 4, 0), 0.0)
                to[OFF + p + 8, OWN - 8 : OWN] = jnp.where(sub >= 4, lower, 0.0)
                to[OFF + p, OWN + 32 : OWN + 40] = jnp.where(sub < 4, upper, 0.0)
                to[OFF + p + 8, OWN + 32 : OWN + 40] = jnp.where(sub < 4, pltpu.roll(upper, 4, 0), 0.0)
        return 0

    lax.fori_loop(0, 3, assemble, 0)

    lane = lax.broadcasted_iota(jnp.int32, (8, 128), 1)
    group = lane >> 2

    def rows(o):
        return pl.ds(pl.multiple_of(LO + 8 * o, 8), 8), pl.ds(pl.multiple_of(8 * o, 8), 8)

    def strips(i, _, source, base):
        comp, o = i // 6, i % 6
        here, to = rows(o)
        first, last = (jnp.zeros((8, 128), f32),) * 2
        for x in range(16):
            t = source[comp, OFF + x, here, :]
            first = jnp.where(group == 2 * x + 1, pltpu.roll(t, 8 * x + 4, 1), first)
            last = jnp.where(group == 2 * x, pltpu.roll(t, (8 * x + 4) % 128, 1), last)
        low[comp + base, to, :] = first
        high[comp + base, to, :] = last
        return 0

    lax.fori_loop(0, 18, lambda i, c: strips(i, c, field, 0), 0)
    lax.fori_loop(0, 36, lambda i, c: strips(i, c, coef, 3), 0)

    def corrected(i, _):
        which, o = i // 6, i % 6
        here, to = rows(o)
        last = jnp.zeros((8, 128), f32)
        for x in range(16):
            t = coef[4 - which, OFF + x, here, :]
            last = jnp.where(lane == 8 * x, pltpu.roll(t, (8 * x + 5) % 128, 1), last)
        high[3 + which, to, :] = high[3 + which, to, :] + last
        return 0

    lax.fori_loop(0, 12, corrected, 0)


def main(field0, coef, zown_low, zown_high, zlow, zhigh, vectors, precond, partial, sink,
         field, diag, node, s, phi, g, fieldS, coefS, diagS, nodeS, sS, phiS, gS):
    f32 = jnp.float32
    lane = lax.broadcasted_iota(jnp.int32, (ROWS, 128), 1)
    first_lane, last_lane = lane == 0, lane == 127

    def at(ref, dy=0):
        return ref[pl.ds(LO + dy, ROWS), :]

    def put(ref, value):
        ref[pl.ds(LO, ROWS), :] = value

    def z_up(value, strip, x):
        return jnp.where(last_lane, pltpu.roll(strip, (123 - 8 * x) & 127, 1), pltpu.roll(value, 127, 1))

    def z_down(value, strip, x):
        return jnp.where(first_lane, pltpu.roll(strip, (125 - 8 * x) & 127, 1), pltpu.roll(value, 1, 1))

    def clear(x, _):
        for c in range(3):
            put(field.at[2, c, x], jnp.zeros((ROWS, 128), f32))
            put(field.at[0, c, x], at(field0.at[c, x]))
        return 0

    lax.fori_loop(0, X, clear, 0)
    for t in range(2):
        own, other = ((zown_low, zlow), (zown_high, zhigh))[t]
        for comp in range(3):
            put(fieldS.at[0, comp, t], own[comp] + other[comp])
            put(fieldS.at[2, comp, t], jnp.zeros((ROWS, 128), f32))
        for comp in range(6):
            put(coefS.at[comp, t], own[comp + 3] + other[comp + 3])

    def diagonals(m, c, cy, cx, cz, mx, my, mz):
        d0 = m[0] + c[1] + cz[1] + c[2] + cy[2]
        d1 = m[1] + c[2] + cx[2] + c[0] + cz[0]
        d2 = m[2] + c[0] + cy[0] + c[1] + cx[1]
        dn = m[0] + mx + m[1] + my + m[2] + mz
        return 1.0 / d0, 1.0 / d1, 1.0 / d2, 1.0 / dn

    def setup_strip(t, _):
        m = [at(coefS.at[c, t]) for c in range(3)]
        c_ = [at(coefS.at[3 + c, t]) for c in range(3)]
        cy = [at(coefS.at[3 + c, t], -1) for c in range(3)]
        cx = [jnp.where(lane < 8, 0.0, pltpu.roll(v, 8, 1)) for v in c_]
        cz = [jnp.where((lane & 7) == 0, 0.0, pltpu.roll(v, 1, 1)) for v in c_]
        out = diagonals(m, c_, cy, cx, cz, pltpu.roll(m[0], 8, 1), at(coefS.at[1, t], -1), pltpu.roll(m[2], 1, 1))
        for c in range(3):
            put(diagS.at[c, t], out[c])
        put(nodeS.at[t], out[3])
        return 0

    lax.fori_loop(0, 2, setup_strip, 0)

    def setup(x, _):
        i = x + OFF
        m = [at(coef.at[c, i]) for c in range(3)]
        c_ = [at(coef.at[3 + c, i]) for c in range(3)]
        cy = [at(coef.at[3 + c, i], -1) for c in range(3)]
        cx = [at(coef.at[3 + c, i - 1]) for c in range(3)]
        cz = [z_down(c_[c], at(coefS.at[3 + c, 0]), x) for c in range(2)]
        out = diagonals(m, c_, cy, cx, cz, at(coef.at[0, i - 1]), at(coef.at[1, i], -1),
                        z_down(m[2], at(coefS.at[2, 0]), x))
        for c in range(3):
            put(diag.at[c, i], out[c])
        put(node.at[i], out[3])
        return 0

    lax.fori_loop(0, 16, setup, 0)

    def fluxes(coefs, e, e0y, e0z, e1x, e1z, e2x, e2y):
        return (coefs[0] * ((e2y - e[2]) - (e1z - e[1])),
                coefs[1] * ((e0z - e[0]) - (e2x - e[2])),
                coefs[2] * ((e1x - e[1]) - (e0y - e[0])))

    def curl_back(gv, g0y, g0z, g1x, g1z, g2x, g2y):
        return ((g1z - gv[1]) - (g2y - gv[2]), (g2x - gv[2]) - (g0z - gv[0]), (g0y - gv[0]) - (g1x - gv[1]))

    def operator_step(k, turns):
        now, later, before = turns
        weight = jnp.where(k == 0, 0.0, jnp.where(k == 1, 0.5, 0.25))

        def strip_first(t, _):
            r = [at(fieldS.at[now, c, t]) for c in range(3)]
            q = ((pltpu.roll(r[0], 8, 1) - r[0]) + (at(fieldS.at[now, 1, t], -1) - r[1])) + (pltpu.roll(r[2], 1, 1) - r[2])
            put(phiS.at[t], q * at(nodeS.at[t]))
            for c in range(3):
                put(sS.at[c, t], r[c] * at(diagS.at[c, t]))
            return 0

        def strip_second(t, _):
            e = [at(sS.at[c, t]) for c in range(3)]
            out = fluxes([at(coefS.at[3 + c, t]) for c in range(3)], e,
                         at(sS.at[0, t], 1), pltpu.roll(e[0], 127, 1), pltpu.roll(e[1], 120, 1),
                         pltpu.roll(e[1], 127, 1), pltpu.roll(e[2], 120, 1), at(sS.at[2, t], 1))
            for c in range(3):
                put(gS.at[c, t], out[c])
            return 0

        def strip_third(t, _):
            gv = [at(gS.at[c, t]) for c in range(3)]
            w = curl_back(gv, at(gS.at[0, t], -1), pltpu.roll(gv[0], 1, 1), pltpu.roll(gv[1], 8, 1),
                          pltpu.roll(gv[1], 1, 1), pltpu.roll(gv[2], 8, 1), at(gS.at[2, t], -1))
            p = at(phiS.at[t])
            up = (pltpu.roll(p, 120, 1), at(phiS.at[t], 1), pltpu.roll(p, 127, 1))
            for c in range(3):
                u = at(sS.at[c, t]) + (up[c] - p)
                put(fieldS.at[later, c, t], (w[c] + at(coefS.at[c, t]) * u - at(fieldS.at[now, c, t]))
                    - weight * at(fieldS.at[before, c, t]))
            return 0

        for part in (strip_first, strip_second, strip_third):
            lax.fori_loop(0, 2, part, 0)

        def row(n_row, sums):
            i = n_row + k + 1
            x = i - OFF
            g_own = [at(g.at[c, i]) for c in range(3)]
            g_x = [at(g.at[c, i - 1]) for c in (1, 2)]
            g_y = [at(g.at[c, i], -1) for c in (0, 2)]
            p, p_x, p_y = at(phi.at[i]), at(phi.at[i + 1]), at(phi.at[i], 1)
            s_own = [at(s.at[c, i]) for c in range(3)]
            r = [at(field.at[now, c, i]) for c in range(3)]
            old = [at(field.at[before, c, i]) for c in range(3)]
            mass = [at(coef.at[c, i]) for c in range(3)]
            a = i + 1
            e = [at(s.at[c, a]) for c in range(3)]
            e_x = [at(s.at[c, a + 1]) for c in (1, 2)]
            e_y = [at(s.at[c, a], 1) for c in (0, 2)]
            curl = [at(coef.at[3 + c, a]) for c in range(3)]
            b = i + 3
            f = [at(field.at[now, c, b]) for c in range(3)]
            f_x, f_y = at(field.at[now, 0, b - 1]), at(field.at[now, 1, b], -1)
            inverse, inverse_node = [at(diag.at[c, b]) for c in range(3)], at(node.at[b])

            w = curl_back(g_own, g_y[0], z_down(g_own[0], at(gS.at[0, 0]), x), g_x[0],
                          z_down(g_own[1], at(gS.at[1, 0]), x), g_x[1], g_y[1])
            up = (p_x, p_y, z_up(p, at(phiS.at[1]), x))
            u = [s_own[c] + (up[c] - p) for c in range(3)]
            v = [((w[c] + mass[c] * u[c]) - r[c]) - weight * old[c] for c in range(3)]
            flux = fluxes(curl, e, e_y[0], z_up(e[0], at(sS.at[0, 1]), x + 1), e_x[0],
                          z_up(e[1], at(sS.at[1, 1]), x + 1), e_x[1], e_y[1])
            q = ((f_x - f[0]) + (f_y - f[1])) + (z_down(f[2], at(fieldS.at[now, 2, 0]), x + 3) - f[2])
            potential = q * inverse_node
            scaled = [f[c] * inverse[c] for c in range(3)]

            inside = (x >= 4) & (x < 12)
            to = jnp.where(inside, x - 4, 8)
            for c in range(3):
                put(field.at[later, c, i], v[c])
                put(g.at[c, a], flux[c])
                put(s.at[c, b], scaled[c])
            put(phi.at[b], potential)
            sums = list(sums)
            for c in range(3):
                uo, ro, vo = (z[OWN - LO : OWN - LO + 32] for z in (u[c], r[c], v[c]))
                vectors[k, c, to] = vo
                precond[k, c, to] = uo
                for n, prod in ((0, ro * uo), (1, vo * uo)):
                    part = (prod[0:8] + prod[8:16]) + (prod[16:24] + prod[24:32])
                    sums[n] = sums[n] + jnp.where(inside, part, 0.0)
            return tuple(sums)

        zero = jnp.zeros((8, 128), f32)
        sums = lax.fori_loop(0, 18 - 2 * k, row, (zero, zero))
        partial[2 * k] = sums[0]
        partial[2 * k + 1] = sums[1]
        return later, before, now

    lax.fori_loop(0, 4, operator_step, (jnp.int32(0), jnp.int32(1), jnp.int32(2)))

    def look(x, _):
        for c in range(3):
            sink[x, c] = s[c, x + OFF, 16:24] + g[c, x + OFF, 16:24]
        sink[x, 3] = phi[x + OFF, 16:24]
        return 0

    lax.fori_loop(0, 2, look, 0)


def fold(partial, out):
    lane = lax.broadcasted_iota(jnp.int32, (1, 128), 1)
    row = jnp.zeros((1, 128), jnp.float32)
    for d in range(8):
        t = jnp.sum(partial[d], axis=0, keepdims=True)
        for shift in (64, 32, 16):
            t = t + pltpu.roll(t, shift, 1)
        row = jnp.where(lane // 16 == d, t, row)
    out[...] = jnp.broadcast_to(row, out.shape)


def finish(everyone, own, vectors, precond, solution_out, residual_out):
    total = jnp.sum(everyone[...], axis=0, keepdims=True)
    lane = lax.broadcasted_iota(jnp.int32, (1, 128), 1)
    dots = [jnp.broadcast_to(jnp.sum(jnp.where(lane // 16 == d, total, 0.0), axis=1, keepdims=True), (8, 128))
            for d in range(8)]
    size = [1.0] + [2.0 ** (1 - k) for k in range(1, 9)]
    moment = [dots[0], dots[1]]
    for k in range(1, 4):
        moment.append((dots[2 * k] * (2.0 / size[k] ** 2) - moment[0]) * size[2 * k])
        moment.append((dots[2 * k + 1] * (2.0 / (size[k] * size[k + 1])) - moment[1]) * size[2 * k + 1])
    row, earlier = moment, None
    alpha, beta = [row[1] / row[0]], [None]
    for k in range(1, 4):
        following = [None] * 8
        for l in range(k, 8 - k):
            t = row[l + 1] - alpha[k - 1] * row[l] + WEIGHT[l if l < 2 else 2] * row[l - 1]
            if k > 1:
                t = t - beta[k - 1] * earlier[l]
            following[l] = t
        alpha.append(following[k + 1] / following[k] - row[k] / row[k - 1])
        beta.append(following[k] / row[k - 1])
        row, earlier = following, row
    zero = jnp.zeros((8, 128), jnp.float32)
    older, newer = [zero] * 6, [zero + 1.0] + [zero] * 5
    value_older, value = zero, zero + 1.0
    weight = lambda l: WEIGHT[min(l, 2)]
    for k in range(4):
        nxt = []
        for l in range(6):
            t = -alpha[k] * newer[l]
            if l > 0:
                t = t + newer[l - 1]
            if l < 5:
                t = t + weight(l + 1) * newer[l + 1]
            if k > 0:
                t = t - beta[k] * older[l]
            nxt.append(t)
        step = (-1.0 - alpha[k]) * value
        if k > 0:
            step = step - beta[k] * value_older
        older, newer, value_older, value = newer, nxt, value, step
    inverse = 1.0 / value
    e = [newer[l] * inverse for l in range(5)]
    S = [None] * 4
    S[3] = -e[4]
    S[2] = -e[3] - S[3]
    S[1] = -e[2] - S[2] - weight(3) * S[3]
    S[0] = -e[1] - S[1] - weight(2) * S[2]
    e = [v[0:1] for v in e]
    S = [v[0:1] for v in S]

    def combine(x, _):
        for c in range(3):
            residual_out[c, x] = (e[0] * own[c, x] + e[1] * vectors[0, c, x]) + (
                e[2] * vectors[1, c, x] + e[3] * vectors[2, c, x]) + e[4] * vectors[3, c, x]
            solution_out[c, x] = (S[0] * precond[0, c, x] + S[1] * precond[1, c, x]) + (
                S[2] * precond[2, c, x] + S[3] * precond[3, c, x])
        return 0

    lax.fori_loop(0, 8, combine, 0)


def shape(*dims):
    return jax.ShapeDtypeStruct(dims, jnp.float32)


def call(kernel, outs, ins, mib, scratch=(), flops=1000000):
    return pl.pallas_call(
        kernel, out_shape=outs, in_specs=[VMEM] * len(ins), out_specs=jax.tree.map(lambda _: VMEM, outs),
        scratch_shapes=list(scratch), compiler_params=pltpu.CompilerParams(vmem_limit_bytes=int(mib * 2**20)),
        cost_estimate=pl.CostEstimate(flops=flops, bytes_accessed=1 << 20, transcendentals=0))(*ins)


def exchange(low, high, axis):
    n = lax.axis_size(axis)
    up = [(i, (i + 1) % n) for i in range(n)]
    return lax.ppermute(high, axis, up), lax.ppermute(low, axis, [(j, i) for i, j in up])


def body(right, mass, curl):
    face = (shape(3, 8, 32, 128),) + (shape(3, 4, 32, 128),) * 2
    b, *ends = call(load, face, (right,), 8)
    b = (b,) + exchange(*ends, "gx")
    c, *ends = call(load, face, (curl,), 8)
    c = (c,) + exchange(*ends, "gx")
    m, *ends = call(load_mass, face, (mass, c[0]), 8)
    block = b + (m,) + exchange(*ends, "gx") + c
    low, high = call(pack_y, (shape(9, 8, 8, 128),) * 2, block, 8)
    block += exchange(low, high, "gy")
    low, high, field, coef = call(
        pack_z, (shape(9, ROWS, 128),) * 2 + (shape(3, X, Y, 128), shape(6, X, Y, 128)), block, 20)
    sides = (low, high) + exchange(low, high, "gz")

    def held(*dims):
        return pltpu.VMEM(dims + (Y, 128), jnp.float32)

    vectors, precond, partial, _ = call(
        main, (shape(4, 3, 9, 32, 128), shape(4, 3, 9, 32, 128), shape(8, 8, 128), shape(2, 4, 8, 128)), (field, coef) + sides, 40,
        [held(3, 3, X), held(3, X), held(X), held(3, X), held(X), held(3, X),
         held(3, 3, 2), held(6, 2), held(3, 2), held(2), held(3, 2), held(2), held(3, 2)])
    axes = ("gx", "gy", "gz")
    devices = lax.axis_size(axes)
    (rows,) = call(fold, (shape(devices, 128),), (partial,), 4)
    everyone = lax.all_to_all(rows.reshape(devices, 1, 128), axes, 0, 0, tiled=True).reshape(devices, 128)
    return call(finish, (shape(3, 8, 32, 128),) * 2, (everyone, b[0], vectors, precond), 16)


def solution(mesh):
    spec = P(None, "gx", "gy", "gz")
    return jax.shard_map(body, mesh=mesh, in_specs=(spec,) * 3, out_specs=(spec,) * 2, check_vma=False)
```

time: 91.4 us -> 75.7 us (0.83)
  Pallas kernels: 32.9 us -> 22.7 us
  waiting for transfers between devices: 22.3 us -> 14.4 us
  starting transfers between devices: 11 us -> 16.4 us
  local copies, waits for them, and re-layouts: 5.98 us -> 2.98 us
    pallas_call x6 -> x8, Pallas kernels: 32.9 us -> 22.7 us  [call(): pl.pallas_call(kernel, out_shape=outs, in_specs=[VMEM] * len(ins), out_sp...]
    ppermute x3 -> x5, waiting for transfers between devices: 18.4 us -> 10 us  [exchange(): lax.ppermute(high, axis, up)]
    ppermute x3 -> x5, starting transfers between devices: 5.67 us -> 11.2 us  [exchange(): lax.ppermute(low, axis, [(j, i) for i, j in up])]
    unnamed x18 -> x6, local copies, waits for them, and re-layouts: 5.98 us -> 2.98 us
    ppermute x3 -> x5, waiting for transfers between devices: 3.89 us -> 4.33 us  [exchange(): lax.ppermute(low, axis, [(j, i) for i, j in up])]
    ppermute x3 -> x5, starting transfers between devices: 5.28 us -> 5.27 us  [exchange(): lax.ppermute(high, axis, up)]
  transfers between devices with their start and end apart: 6 -> 10, of which waited for: 3 -> 6; matrix products, arithmetic and copies ran while one was open for 0% -> 0% of each run, Pallas kernels for 0% -> 0%
where the time goes in v1:
time: 75.7 us; the launch traced here: 75.5 us
  Pallas kernels  22.7 us (30%)
  blocking collectives  18.3 us (24%)
  starting transfers between devices  16.4 us (22%)
  waiting for transfers between devices  14.4 us (19%)
  local copies, waits for them, and re-layouts  2.98 us (4%)
    pallas_call x8, Pallas kernels, call(): pl.pallas_call(kernel, out_shape=outs, in_specs=[VMEM] * len(ins), out_sp...  22.7 us
    all_to_all x1, blocking collectives, body(): lax.all_to_all(rows.reshape(devices, 1, 128), axes, 0, 0, tiled=True)  18.3 us
    ppermute x5, starting transfers between devices, exchange(): lax.ppermute(low, axis, [(j, i) for i, j in up])  11.2 us
    ppermute x5, waiting for transfers between devices, exchange(): lax.ppermute(high, axis, up)  10 us
    ppermute x5, starting transfers between devices, exchange(): lax.ppermute(high, axis, up)  5.27 us
    ppermute x5, waiting for transfers between devices, exchange(): lax.ppermute(low, axis, [(j, i) for i, j in up])  4.33 us
    unnamed x6, local copies, waits for them, and re-layouts  2.98 us
  transfers between devices with their start and end apart: 10, of which 6 were waited for; matrix products, arithmetic and copies ran while one was open for 0% of the time, Pallas kernels for 0%

profile of v1, /device:TPU:1, one launch (start us, length us, event | category | flops | bytes accessed | tf_op | source)
XLA Modules:
  0.0 75.5 jit_solution(1174821246453273365)
XLA Ops:
  0.6 1.0 %copy-done = f32[3,8,32,128]{3,2,1,0:T(8,128)S(1)} copy-done((f32[3,8,32,128]{3,2,1,0:T(8,128)S(1)}, f32[3,8,32,128]{3,2,1,0:T(8,128)}, u32[]{:S(2)}) %copy-start) | copy-done | bytes 393240
  1.7 2.1 %collective-permute-start = (f32[3,4,32,128]{3,2,1,0:T(8,128)S(1)}, f32[3,4,32,128]{3,2,1,0:T(8,128)S(1)}, u32[]{:S(2)}, u32[]{:S(2)}) collective-permute-start(f32[3,4,32,128]{3,2,1,0:T(8,128)S(1)} %get-tuple-element.21), channel_id=1, source_target_pairs={{0,32},{32,64},{64,96},{96,0},{1,33},{33,65},{65,97},{97,1},{2,34}... | collective-permute-start | bytes 589832 | tf_op jit(solution)/shard_map/ppermute | solution.py:394
  3.8 1.3 %collective-permute-start.1 = (f32[3,4,32,128]{3,2,1,0:T(8,128)S(1)}, f32[3,4,32,128]{3,2,1,0:T(8,128)S(1)}, u32[]{:S(2)}, u32[]{:S(2)}) collective-permute-start(f32[3,4,32,128]{3,2,1,0:T(8,128)S(1)} %get-tuple-element.22), channel_id=1, source_target_pairs={{32,0},{64,32},{96,64},{0,96},{33,1},{65,33},{97,65},{1,97},{34,2}... | collective-permute-start | bytes 589832 | tf_op jit(solution)/shard_map/ppermute | solution.py:394
  5.1 1.0 %copy-done.1 = f32[3,8,32,128]{3,2,1,0:T(8,128)S(1)} copy-done((f32[3,8,32,128]{3,2,1,0:T(8,128)S(1)}, f32[3,8,32,128]{3,2,1,0:T(8,128)}, u32[]{:S(2)}) %copy-start.1) | copy-done | bytes 393240
  6.2 0.2 collective-permute-start.4
  6.4 2.6 %collective-permute-start.5 = (f32[3,4,32,128]{3,2,1,0:T(8,128)S(1)}, f32[3,4,32,128]{3,2,1,0:T(8,128)S(1)}, u32[]{:S(2)}, u32[]{:S(2)}) collective-permute-start(f32[3,4,32,128]{3,2,1,0:T(8,128)S(1)} %get-tuple-element.28), channel_id=1, source_target_pairs={{32,0},{64,32},{96,64},{0,96},{33,1},{65,33},{97,65},{1,97},{34,2}... | collective-permute-start | bytes 589832 | tf_op jit(solution)/shard_map/ppermute | solution.py:394
  8.9 1.0 %copy-done.2 = f32[3,8,32,128]{3,2,1,0:T(8,128)S(1)} copy-done((f32[3,8,32,128]{3,2,1,0:T(8,128)S(1)}, f32[3,8,32,128]{3,2,1,0:T(8,128)}, u32[]{:S(2)}) %copy-start.2) | copy-done | bytes 393240
  10.1 2.7 %collective-permute-start.3 = (f32[3,4,32,128]{3,2,1,0:T(8,128)S(1)}, f32[3,4,32,128]{3,2,1,0:T(8,128)S(1)}, u32[]{:S(2)}, u32[]{:S(2)}) collective-permute-start(f32[3,4,32,128]{3,2,1,0:T(8,128)S(1)} %get-tuple-element.26), channel_id=1, source_target_pairs={{32,0},{64,32},{96,64},{0,96},{33,1},{65,33},{97,65},{1,97},{34,2}... | collective-permute-start | bytes 589832 | tf_op jit(solution)/shard_map/ppermute | solution.py:394
  12.7 0.6 collective-permute-done.4.refs_7_
  13.4 0.1 collective-permute-done.5.refs_8_
  13.5 3.9 %collective-permute-done.2.refs_4_ = f32[3,4,32,128]{3,2,1,0:T(8,128)S(1)} collective-permute-done((f32[3,4,32,128]{3,2,1,0:T(8,128)S(1)}, f32[3,4,32,128]{3,2,1,0:T(8,128)S(1)}, u32[]{:S(2)}, u32[]{:S(2)}) %collective-permute-start.2) | collective-permute-done | bytes 196640 | tf_op jit(solution)/shard_map/ppermute | solution.py:394
  17.4 0.3 collective-permute-done.3.refs_5_
  17.7 0.1 shard_map.53
  17.8 1.7 %collective-permute-start.6 = (f32[9,8,8,128]{3,2,1,0:T(8,128)S(1)}, f32[9,8,8,128]{3,2,1,0:T(8,128)S(1)}, u32[]{:S(2)}, u32[]{:S(2)}) collective-permute-start(f32[9,8,8,128]{3,2,1,0:T(8,128)S(1)} %get-tuple-element.29), channel_id=1, source_target_pairs={{0,8},{8,16},{16,24},{24,0},{1,9},{9,17},{17,25},{25,1},{2,10},{10... | collective-permute-start | bytes 884744 | tf_op jit(solution)/shard_map/ppermute | solution.py:394
  19.5 2.2 %collective-permute-start.7 = (f32[9,8,8,128]{3,2,1,0:T(8,128)S(1)}, f32[9,8,8,128]{3,2,1,0:T(8,128)S(1)}, u32[]{:S(2)}, u32[]{:S(2)}) collective-permute-start(f32[9,8,8,128]{3,2,1,0:T(8,128)S(1)} %get-tuple-element.30), channel_id=1, source_target_pairs={{8,0},{16,8},{24,16},{0,24},{9,1},{17,9},{25,17},{1,25},{10,2},{18... | collective-permute-start | bytes 884744 | tf_op jit(solution)/shard_map/ppermute | solution.py:394
  21.7 5.5 %collective-permute-done.6.refs_9_ = f32[9,8,8,128]{3,2,1,0:T(8,128)S(1)} collective-permute-done((f32[9,8,8,128]{3,2,1,0:T(8,128)S(1)}, f32[9,8,8,128]{3,2,1,0:T(8,128)S(1)}, u32[]{:S(2)}, u32[]{:S(2)}) %collective-permute-start.6) | collective-permute-done | bytes 294944 | tf_op jit(solution)/shard_map/ppermute | solution.py:394
  27.2 6.3 %shard_map.54 = (f32[9,48,128]{2,1,0:T(8,128)S(1)}, f32[9,48,128]{2,1,0:T(8,128)S(1)}, f32[3,24,64,128]{3,2,1,0:T(8,128)S(1)}, f32[6,24,64,128]{3,2,1,0:T(8,128)S(1)}) custom-call(f32[3,8,32,128]{3,2,1,0:T(8,128)S(1)} %get-tuple-element.20.refs_0_.own, f32[3,4,32,128]{3,2,1,0:T(8,128)S(1)} %collective-permute-done.refs_1_, ...), custom_call_target="tpu_custom_call" | custom-call | flops 1000000 | bytes 1048576 | tf_op jit(solution)/shard_map/pallas_call | solution.py:385
  33.5 2.4 %collective-permute-start.9 = (f32[9,48,128]{2,1,0:T(8,128)S(1)}, f32[9,48,128]{2,1,0:T(8,128)S(1)}, u32[]{:S(2)}, u32[]{:S(2)}) collective-permute-start(f32[9,48,128]{2,1,0:T(8,128)S(1)} %get-tuple-element.33.zown_low), channel_id=1, source_target_pairs={{1,0},{2,1},{3,2},{4,3},{5,4},{6,5},{7,6},{0,7},{9,8},{10,9},{11,1... | collective-permute-start | bytes 663560 | tf_op jit(solution)/shard_map/ppermute | solution.py:394
  35.9 1.2 %collective-permute-start.8 = (f32[9,48,128]{2,1,0:T(8,128)S(1)}, f32[9,48,128]{2,1,0:T(8,128)S(1)}, u32[]{:S(2)}, u32[]{:S(2)}) collective-permute-start(f32[9,48,128]{2,1,0:T(8,128)S(1)} %get-tuple-element.34.zown_high), channel_id=1, source_target_pairs={{0,1},{1,2},{2,3},{3,4},{4,5},{5,6},{6,7},{7,0},{8,9},{9,10},{10,1... | collective-permute-start | bytes 663560 | tf_op jit(solution)/shard_map/ppermute | solution.py:394
  37.1 3.9 %collective-permute-done.9.zhigh = f32[9,48,128]{2,1,0:T(8,128)S(1)} collective-permute-done((f32[9,48,128]{2,1,0:T(8,128)S(1)}, f32[9,48,128]{2,1,0:T(8,128)S(1)}, u32[]{:S(2)}, u32[]{:S(2)}) %collective-permute-start.9) | collective-permute-done | bytes 221216 | tf_op jit(solution)/shard_map/ppermute | solution.py:394
  41.0 14.7 %shard_map.55 = (f32[4,3,9,32,128]{4,3,2,1,0:T(8,128)S(1)}, f32[4,3,9,32,128]{4,3,2,1,0:T(8,128)S(1)}, f32[8,8,128]{2,1,0:T(8,128)S(1)}, f32[2,4,8,128]{3,2,1,0:T(8,128)}) custom-call(f32[3,24,64,128]{3,2,1,0:T(8,128)S(1)} %get-tuple-element.31.field0, f32[6,24,64,128]{3,2,1,0:T(8,128)S(1)} %get-tuple-element.32.coef, ...), custom_call_target="tpu_custom_call" | custom-call | flops 1000000 | bytes 1048576 | tf_op jit(solution)/shard_map/pallas_call | solution.py:385
  55.7 0.2 shard_map.56
  55.9 18.3 %all_to_all.5 = f32[128,1,128]{2,1,0:T(1,128)S(1)} all-to-all(f32[128,1,128]{2,1,0:T(1,128)S(1)} %bitcast.5), channel_id=1, replica_groups=mesh['gx'=4,'gy'=4,'gz'=8] {'gx','gy','gz'}, dimensions={0} | all-to-all | bytes 131072 | tf_op jit(solution)/shard_map/all_to_all | solution.py:421
  74.2 1.3 %shard_map.57 = (f32[3,8,32,128]{3,2,1,0:T(8,128)}, f32[3,8,32,128]{3,2,1,0:T(8,128)}) custom-call(f32[128,128]{1,0:T(8,128)S(1)} %bitcast.4, f32[3,8,32,128]{3,2,1,0:T(8,128)S(1)} %get-tuple-element.20.refs_0_.own, f32[4,3,9,32,128]{4,3,2,1,0:T(8,128)S(1)} %get-tuple-element.36.vectors, f32[4,3,9,32,128]{4,3,2,1,0:T(8,128)S(1)} %get-tuple-element.37.precond), custom_call_target="tpu_custom_call" | custom-call | flops 1000000 | bytes 1048576 | tf_op jit(solution)/shard_map/pallas_call | solution.py:385
  (11 shorter events, 0.3 us)
Async XLA Ops:
  0.6 1.0 %copy-start = (f32[3,8,32,128]{3,2,1,0:T(8,128)S(1)}, f32[3,8,32,128]{3,2,1,0:T(8,128)}, u32[]{:S(2)}) copy-start(f32[3,8,32,128]{3,2,1,0:T(8,128)} %source.3) | copy-start | bytes 1179652
  1.7 8.4 %collective-permute-start = (f32[3,4,32,128]{3,2,1,0:T(8,128)S(1)}, f32[3,4,32,128]{3,2,1,0:T(8,128)S(1)}, u32[]{:S(2)}, u32[]{:S(2)}) collective-permute-start(f32[3,4,32,128]{3,2,1,0:T(8,128)S(1)} %get-tuple-element.21), channel_id=1, source_target_pairs={{0,32},{32,64},{64,96},{96,0},{1,33},{33,65},{65,97},{97,1},{2,34}... | collective-permute-start | bytes 589832 | tf_op jit(solution)/shard_map/ppermute | solution.py:394
  3.8 9.0 %collective-permute-start.1 = (f32[3,4,32,128]{3,2,1,0:T(8,128)S(1)}, f32[3,4,32,128]{3,2,1,0:T(8,128)S(1)}, u32[]{:S(2)}, u32[]{:S(2)}) collective-permute-start(f32[3,4,32,128]{3,2,1,0:T(8,128)S(1)} %get-tuple-element.22), channel_id=1, source_target_pairs={{32,0},{64,32},{96,64},{0,96},{33,1},{65,33},{97,65},{1,97},{34,2}... | collective-permute-start | bytes 589832 | tf_op jit(solution)/shard_map/ppermute | solution.py:394
  5.1 1.0 %copy-start.1 = (f32[3,8,32,128]{3,2,1,0:T(8,128)S(1)}, f32[3,8,32,128]{3,2,1,0:T(8,128)}, u32[]{:S(2)}) copy-start(f32[3,8,32,128]{3,2,1,0:T(8,128)} %source.4) | copy-start | bytes 1179652
  6.2 7.2 %collective-permute-start.4 = (f32[3,4,32,128]{3,2,1,0:T(8,128)S(1)}, f32[3,4,32,128]{3,2,1,0:T(8,128)S(1)}, u32[]{:S(2)}, u32[]{:S(2)}) collective-permute-start(f32[3,4,32,128]{3,2,1,0:T(8,128)S(1)} %get-tuple-element.27), channel_id=1, source_target_pairs={{0,32},{32,64},{64,96},{96,0},{1,33},{33,65},{65,97},{97,1},{2,34}... | collective-permute-start | bytes 589832 | tf_op jit(solution)/shard_map/ppermute | solution.py:394
  6.4 7.1 %collective-permute-start.5 = (f32[3,4,32,128]{3,2,1,0:T(8,128)S(1)}, f32[3,4,32,128]{3,2,1,0:T(8,128)S(1)}, u32[]{:S(2)}, u32[]{:S(2)}) collective-permute-start(f32[3,4,32,128]{3,2,1,0:T(8,128)S(1)} %get-tuple-element.28), channel_id=1, source_target_pairs={{32,0},{64,32},{96,64},{0,96},{33,1},{65,33},{97,65},{1,97},{34,2}... | collective-permute-start | bytes 589832 | tf_op jit(solution)/shard_map/ppermute | solution.py:394
  8.9 1.0 %copy-start.2 = (f32[3,8,32,128]{3,2,1,0:T(8,128)S(1)}, f32[3,8,32,128]{3,2,1,0:T(8,128)}, u32[]{:S(2)}) copy-start(f32[3,8,32,128]{3,2,1,0:T(8,128)} %source.5) | copy-start | bytes 1179652
  10.0 7.4 %collective-permute-start.2 = (f32[3,4,32,128]{3,2,1,0:T(8,128)S(1)}, f32[3,4,32,128]{3,2,1,0:T(8,128)S(1)}, u32[]{:S(2)}, u32[]{:S(2)}) collective-permute-start(f32[3,4,32,128]{3,2,1,0:T(8,128)S(1)} %get-tuple-element.25), channel_id=1, source_target_pairs={{0,32},{32,64},{64,96},{96,0},{1,33},{33,65},{65,97},{97,1},{2,34}... | collective-permute-start | bytes 589832 | tf_op jit(solution)/shard_map/ppermute | solution.py:394
  10.1 7.6 %collective-permute-start.3 = (f32[3,4,32,128]{3,2,1,0:T(8,128)S(1)}, f32[3,4,32,128]{3,2,1,0:T(8,128)S(1)}, u32[]{:S(2)}, u32[]{:S(2)}) collective-permute-start(f32[3,4,32,128]{3,2,1,0:T(8,128)S(1)} %get-tuple-element.26), channel_id=1, source_target_pairs={{32,0},{64,32},{96,64},{0,96},{33,1},{65,33},{97,65},{1,97},{34,2}... | collective-permute-start | bytes 589832 | tf_op jit(solution)/shard_map/ppermute | solution.py:394
  17.8 9.4 %collective-permute-start.6 = (f32[9,8,8,128]{3,2,1,0:T(8,128)S(1)}, f32[9,8,8,128]{3,2,1,0:T(8,128)S(1)}, u32[]{:S(2)}, u32[]{:S(2)}) collective-permute-start(f32[9,8,8,128]{3,2,1,0:T(8,128)S(1)} %get-tuple-element.29), channel_id=1, source_target_pairs={{0,8},{8,16},{16,24},{24,0},{1,9},{9,17},{17,25},{25,1},{2,10},{10... | collective-permute-start | bytes 884744 | tf_op jit(solution)/shard_map/ppermute | solution.py:394
  19.5 7.7 %collective-permute-start.7 = (f32[9,8,8,128]{3,2,1,0:T(8,128)S(1)}, f32[9,8,8,128]{3,2,1,0:T(8,128)S(1)}, u32[]{:S(2)}, u32[]{:S(2)}) collective-permute-start(f32[9,8,8,128]{3,2,1,0:T(8,128)S(1)} %get-tuple-element.30), channel_id=1, source_target_pairs={{8,0},{16,8},{24,16},{0,24},{9,1},{17,9},{25,17},{1,25},{10,2},{18... | collective-permute-start | bytes 884744 | tf_op jit(solution)/shard_map/ppermute | solution.py:394
  33.5 7.5 %collective-permute-start.9 = (f32[9,48,128]{2,1,0:T(8,128)S(1)}, f32[9,48,128]{2,1,0:T(8,128)S(1)}, u32[]{:S(2)}, u32[]{:S(2)}) collective-permute-start(f32[9,48,128]{2,1,0:T(8,128)S(1)} %get-tuple-element.33.zown_low), channel_id=1, source_target_pairs={{1,0},{2,1},{3,2},{4,3},{5,4},{6,5},{7,6},{0,7},{9,8},{10,9},{11,1... | collective-permute-start | bytes 663560 | tf_op jit(solution)/shard_map/ppermute | solution.py:394
  35.9 5.1 %collective-permute-start.8 = (f32[9,48,128]{2,1,0:T(8,128)S(1)}, f32[9,48,128]{2,1,0:T(8,128)S(1)}, u32[]{:S(2)}, u32[]{:S(2)}) collective-permute-start(f32[9,48,128]{2,1,0:T(8,128)S(1)} %get-tuple-element.34.zown_high), channel_id=1, source_target_pairs={{0,1},{1,2},{2,3},{3,4},{4,5},{5,6},{6,7},{7,0},{8,9},{9,10},{10,1... | collective-permute-start | bytes 663560 | tf_op jit(solution)/shard_map/ppermute | solution.py:394

commit v2 on v1

--- a/solution.py
+++ b/solution.py
@@ -30,139 +30,200 @@
     high[2, 0] = source[2, 4] + curl[1, 3]
 
 
-def row_tile(parts, c, x, y):
-    own, below, above = parts
-    if x < 4:
-        return below[c, x, y : y + 8]
-    if x >= 12:
-        return above[c, x - 12, y : y + 8]
-    return own[c, x - 4, y : y + 8]
-
-
-def pack_y(*refs):
-    blocks, (low, high) = (refs[0:3], refs[3:6], refs[6:9]), refs[9:]
+def pack_y(pairs, *refs):
+    refs, (low, high) = refs[:-2], refs[-2:]
+    n = len(refs) // 3
     sub = lax.broadcasted_iota(jnp.int32, (8, 128), 0)
 
+    def tile(field, c, p, half, y):
+        return pairs(refs[field * n : field * n + n], c, p, half, y)
+
     def pack(c, _):
-        for n, parts in enumerate(blocks):
-            for p in range(8):
-                a = row_tile(parts, c, p, 0)
-                b = row_tile(parts, c, p + 8, 0)
-                low[3 * n + c, p] = jnp.where(sub < 4, a, pltpu.roll(b, 4, 0))
-                a = row_tile(parts, c, p, 24)
-                b = row_tile(parts, c, p + 8, 24)
-                high[3 * n + c, p] = jnp.where(sub < 4, pltpu.roll(a, 4, 0), b)
+        for field in range(3):
+            for p in range(4):
+                a, b = tile(field, c, p, 0, 0), tile(field, c, p, 1, 0)
+                low[3 * field + c, p] = jnp.where(sub < 4, a, pltpu.roll(b, 4, 0))
+                a, b = tile(field, c, p, 0, 24), tile(field, c, p, 1, 24)
+                high[3 * field + c, p] = jnp.where(sub < 4, pltpu.roll(a, 4, 0), b)
         return 0
 
     lax.fori_loop(0, 3, pack, 0)
 
     def corrected(i, _):
         c, other = 2 * i, 2 - 2 * i
-        for p in range(8):
-            a = pltpu.roll(row_tile(blocks[2], other, p, 24), 5, 0)
-            b = pltpu.roll(row_tile(blocks[2], other, p + 8, 24), 1, 0)
+        for p in range(4):
+            a = pltpu.roll(tile(2, other, p, 0, 24), 5, 0)
+            b = pltpu.roll(tile(2, other, p, 1, 24), 1, 0)
             high[3 + c, p] = high[3 + c, p] + jnp.where(sub == 0, a, jnp.where(sub == 4, b, 0.0))
         return 0
 
     lax.fori_loop(0, 2, corrected, 0)
 
 
-def pack_z(*refs):
-    blocks, (ylow, yhigh, low, high, field, coef) = (refs[0:3], refs[3:6], refs[6:9]), refs[9:]
-    f32 = jnp.float32
-    sub = lax.broadcasted_iota(jnp.int32, (8, 128), 0)
-
-    def assemble(c, _):
-        for n, (own, below, above) in enumerate(blocks):
-            to = field.at[c] if n == 0 else coef.at[3 * n - 3 + c]
-            if n > 0:
-                to[OFF - 1] = jnp.zeros((Y, 128), f32)
-            to[OFF : OFF + 4, OWN : OWN + 32] = below[c]
-            to[OFF + 4 : OFF + 12, OWN : OWN + 32] = own[c]
-            to[OFF + 12 : OFF + 16, OWN : OWN + 32] = above[c]
-            for p in range(8):
-                lower, upper = ylow[3 * n + c, p], yhigh[3 * n + c, p]
-                to[OFF + p, OWN - 8 : OWN] = jnp.where(sub >= 4, pltpu.roll(lower, 4, 0), 0.0)
-                to[OFF + p + 8, OWN - 8 : OWN] = jnp.where(sub >= 4, lower, 0.0)
-                to[OFF + p, OWN + 32 : OWN + 40] = jnp.where(sub < 4, upper, 0.0)
-                to[OFF + p + 8, OWN + 32 : OWN + 40] = jnp.where(sub < 4, pltpu.roll(upper, 4, 0), 0.0)
-        return 0
-
-    lax.fori_loop(0, 3, assemble, 0)
-
-    lane = lax.broadcasted_iota(jnp.int32, (8, 128), 1)
-    group = lane >> 2
-
-    def rows(o):
-        return pl.ds(pl.multiple_of(LO + 8 * o, 8), 8), pl.ds(pl.multiple_of(8 * o, 8), 8)
-
-    def strips(i, _, source, base):
-        comp, o = i // 6, i % 6
-        here, to = rows(o)
-        first, last = (jnp.zeros((8, 128), f32),) * 2
+def pack_y_own(*refs):
+    pack_y(lambda own, c, p, half, y: own[0][c, p + 4 * half, y : y + 8], *refs)
+
+
+def pack_y_halo(*refs):
+    pack_y(lambda ends, c, p, half, y: ends[half][c, p, y : y + 8], *refs)
+
+
+def strips(source, base, count, octets, low, high):
+    group = lax.broadcasted_iota(jnp.int32, (8, 128), 1) >> 2
+    each, x0, start, begin, stride = octets
+
+    def one(i, _):
+        comp, o = i // each, i % each
+        here = pl.ds(pl.multiple_of(start + 8 * o, 8), 8)
+        to = pl.ds(pl.multiple_of(begin + stride * o, 8), 8)
+        first, last = (jnp.zeros((8, 128), jnp.float32),) * 2
         for x in range(16):
-            t = source[comp, OFF + x, here, :]
+            t = source[comp, x0 + x, here, :]
             first = jnp.where(group == 2 * x + 1, pltpu.roll(t, 8 * x + 4, 1), first)
             last = jnp.where(group == 2 * x, pltpu.roll(t, (8 * x + 4) % 128, 1), last)
         low[comp + base, to, :] = first
         high[comp + base, to, :] = last
         return 0
 
-    lax.fori_loop(0, 18, lambda i, c: strips(i, c, field, 0), 0)
-    lax.fori_loop(0, 36, lambda i, c: strips(i, c, coef, 3), 0)
+    lax.fori_loop(0, count * each, one, 0)
+
+
+def all_strips(field, coef, octets, low, high):
+    strips(field, 0, 3, octets, low, high)
+    strips(coef, 3, 6, octets, low, high)
+    lane = lax.broadcasted_iota(jnp.int32, (8, 128), 1)
+    each, x0, start, begin, stride = octets
 
     def corrected(i, _):
-        which, o = i // 6, i % 6
-        here, to = rows(o)
-        last = jnp.zeros((8, 128), f32)
+        which, o = i // each, i % each
+        here = pl.ds(pl.multiple_of(start + 8 * o, 8), 8)
+        to = pl.ds(pl.multiple_of(begin + stride * o, 8), 8)
+        last = jnp.zeros((8, 128), jnp.float32)
         for x in range(16):
-            t = coef[4 - which, OFF + x, here, :]
+            t = coef[4 - which, x0 + x, here, :]
             last = jnp.where(lane == 8 * x, pltpu.roll(t, (8 * x + 5) % 128, 1), last)
         high[3 + which, to, :] = high[3 + which, to, :] + last
         return 0
 
-    lax.fori_loop(0, 12, corrected, 0)
-
-
-def main(field0, coef, zown_low, zown_high, zlow, zhigh, vectors, precond, partial, sink,
+    lax.fori_loop(0, 2 * each, corrected, 0)
+
+
+def pack_z_middle(*refs):
+    blocks, (low, high, field, coef) = (refs[0:3], refs[3:6], refs[6:9]), refs[9:]
+
+    def assemble(c, _):
+        for n, (own, below, above) in enumerate(blocks):
+            to = field.at[c] if n == 0 else coef.at[3 * n - 3 + c]
+            to[OFF : OFF + 4, OWN : OWN + 32] = below[c]
+            to[OFF + 4 : OFF + 12, OWN : OWN + 32] = own[c]
+            to[OFF + 12 : OFF + 16, OWN : OWN + 32] = above[c]
+        return 0
+
+    lax.fori_loop(0, 3, assemble, 0)
+    all_strips(field, coef, (4, OFF, OWN, 8, 8), low, high)
+
+
+def pack_z_edge(own_low, own_high, halo_low, halo_high, middle_low, middle_high,
+                low, high, send_low, send_high, field, coef):
+    sub = lax.broadcasted_iota(jnp.int32, (8, 128), 0)
+
+    def assemble(c, _):
+        for n in range(3):
+            to = field.at[c] if n == 0 else coef.at[3 * n - 3 + c]
+            comp = 3 * n + c
+            for p in range(4):
+                for lows, highs, x0, x1 in ((halo_low, halo_high, p, p + 12), (own_low, own_high, p + 4, p + 8)):
+                    lower, upper = lows[comp, p], highs[comp, p]
+                    to[x0, 0:8] = jnp.where(sub >= 4, pltpu.roll(lower, 4, 0), 0.0)
+                    to[x1, 0:8] = jnp.where(sub >= 4, lower, 0.0)
+                    to[x0, 8:16] = jnp.where(sub < 4, upper, 0.0)
+                    to[x1, 8:16] = jnp.where(sub < 4, pltpu.roll(upper, 4, 0), 0.0)
+        return 0
+
+    lax.fori_loop(0, 3, assemble, 0)
+    all_strips(field, coef, (2, 0, 0, 0, 40), low, high)
+    for comp in range(9):
+        low[comp, 8:40] = middle_low[comp, 8:40]
+        high[comp, 8:40] = middle_high[comp, 8:40]
+    for n in range(5):
+        down, up = low[n], high[n]
+        if n < 4:
+            down, up = down + pltpu.roll(low[n + 5], 124, 1), up + pltpu.roll(high[n + 5], 4, 1)
+        send_low[n] = down
+        send_high[n] = up
+
+
+def at(ref, dy=0):
+    return ref[pl.ds(LO + dy, ROWS), :]
+
+
+def put(ref, value):
+    ref[pl.ds(LO, ROWS), :] = value
+
+
+def diagonals(m, c, cy, cx, cz, mx, my, mz):
+    d0 = m[0] + c[1] + cz[1] + c[2] + cy[2]
+    d1 = m[1] + c[2] + cx[2] + c[0] + cz[0]
+    d2 = m[2] + c[0] + cy[0] + c[1] + cx[1]
+    dn = m[0] + mx + m[1] + my + m[2] + mz
+    return 1.0 / d0, 1.0 / d1, 1.0 / d2, 1.0 / dn
+
+
+def invert(field_middle, coef_middle, field_edge, coef_edge, field, coef, diag, node):
+    def assemble(c, _):
+        coef[c, OFF - 1] = jnp.zeros((Y, 128), jnp.float32)
+        for x in range(OFF, OFF + 16):
+            coef[c, x, OWN : OWN + 32] = coef_middle[c, x, OWN : OWN + 32]
+            coef[c, x, OWN - 8 : OWN] = coef_edge[c, x - OFF, 0:8]
+            coef[c, x, OWN + 32 : OWN + 40] = coef_edge[c, x - OFF, 8:16]
+        return 0
+
+    def assemble_field(c, _):
+        for x in range(OFF, OFF + 16):
+            field[c, x, OWN : OWN + 32] = field_middle[c, x, OWN : OWN + 32]
+            field[c, x, OWN - 8 : OWN] = field_edge[c, x - OFF, 0:8]
+            field[c, x, OWN + 32 : OWN + 40] = field_edge[c, x - OFF, 8:16]
+        return 0
+
+    lax.fori_loop(0, 6, assemble, 0)
+    lax.fori_loop(0, 3, assemble_field, 0)
+
+    def row(x, _):
+        i = x + OFF
+        m = [at(coef.at[c, i]) for c in range(3)]
+        c_ = [at(coef.at[3 + c, i]) for c in range(3)]
+        cy = [at(coef.at[3 + c, i], -1) for c in range(3)]
+        cx = [at(coef.at[3 + c, i - 1]) for c in range(3)]
+        cz = [pltpu.roll(c_[c], 1, 1) for c in range(2)]
+        out = diagonals(m, c_, cy, cx, cz, at(coef.at[0, i - 1]), at(coef.at[1, i], -1), pltpu.roll(m[2], 1, 1))
+        for c in range(3):
+            put(diag.at[c, i], out[c])
+        put(node.at[i], out[3])
+        return 0
+
+    lax.fori_loop(0, 16, row, 0)
+
+
+def main(field_in, coef, diag_in, node_in, zown_low, zown_high, zlow, zhigh, vectors, precond, partial, sink,
          field, diag, node, s, phi, g, fieldS, coefS, diagS, nodeS, sS, phiS, gS):
     f32 = jnp.float32
     lane = lax.broadcasted_iota(jnp.int32, (ROWS, 128), 1)
     first_lane, last_lane = lane == 0, lane == 127
 
-    def at(ref, dy=0):
-        return ref[pl.ds(LO + dy, ROWS), :]
-
-    def put(ref, value):
-        ref[pl.ds(LO, ROWS), :] = value
-
     def z_up(value, strip, x):
         return jnp.where(last_lane, pltpu.roll(strip, (123 - 8 * x) & 127, 1), pltpu.roll(value, 127, 1))
 
     def z_down(value, strip, x):
         return jnp.where(first_lane, pltpu.roll(strip, (125 - 8 * x) & 127, 1), pltpu.roll(value, 1, 1))
 
-    def clear(x, _):
-        for c in range(3):
-            put(field.at[2, c, x], jnp.zeros((ROWS, 128), f32))
-            put(field.at[0, c, x], at(field0.at[c, x]))
-        return 0
-
-    lax.fori_loop(0, X, clear, 0)
-    for t in range(2):
-        own, other = ((zown_low, zlow), (zown_high, zhigh))[t]
-        for comp in range(3):
-            put(fieldS.at[0, comp, t], own[comp] + other[comp])
-            put(fieldS.at[2, comp, t], jnp.zeros((ROWS, 128), f32))
-        for comp in range(6):
-            put(coefS.at[comp, t], own[comp + 3] + other[comp + 3])
-
-    def diagonals(m, c, cy, cx, cz, mx, my, mz):
-        d0 = m[0] + c[1] + cz[1] + c[2] + cy[2]
-        d1 = m[1] + c[2] + cx[2] + c[0] + cz[0]
-        d2 = m[2] + c[0] + cy[0] + c[1] + cx[1]
-        dn = m[0] + mx + m[1] + my + m[2] + mz
-        return 1.0 / d0, 1.0 / d1, 1.0 / d2, 1.0 / dn
+    upper = (lane & 4) != 0
+    for comp in range(9):
+        lower_part, upper_part = zlow[comp % 5], zhigh[comp % 5]
+        if comp >= 5:
+            lower_part, upper_part = pltpu.roll(lower_part, 124, 1), pltpu.roll(upper_part, 4, 1)
+        for t, value in ((0, jnp.where(upper, zown_low[comp], lower_part)),
+                         (1, jnp.where(upper, upper_part, zown_high[comp]))):
+            put(fieldS.at[0, comp, t] if comp < 3 else coefS.at[comp - 3, t], value)
 
     def setup_strip(t, _):
         m = [at(coefS.at[c, t]) for c in range(3)]
@@ -180,16 +241,10 @@
 
     def setup(x, _):
         i = x + OFF
-        m = [at(coef.at[c, i]) for c in range(3)]
-        c_ = [at(coef.at[3 + c, i]) for c in range(3)]
-        cy = [at(coef.at[3 + c, i], -1) for c in range(3)]
-        cx = [at(coef.at[3 + c, i - 1]) for c in range(3)]
-        cz = [z_down(c_[c], at(coefS.at[3 + c, 0]), x) for c in range(2)]
-        out = diagonals(m, c_, cy, cx, cz, at(coef.at[0, i - 1]), at(coef.at[1, i], -1),
-                        z_down(m[2], at(coefS.at[2, 0]), x))
         for c in range(3):
-            put(diag.at[c, i], out[c])
-        put(node.at[i], out[3])
+            put(field.at[0, c, i], at(field_in.at[c, i]))
+            put(diag.at[c, i], jnp.where(first_lane, pltpu.roll(at(diagS.at[c, 0]), 124 - 8 * x, 1), at(diag_in.at[c, i])))
+        put(node.at[i], jnp.where(first_lane, pltpu.roll(at(nodeS.at[0]), 124 - 8 * x, 1), at(node_in.at[i])))
         return 0
 
     lax.fori_loop(0, 16, setup, 0)
@@ -291,9 +346,9 @@
         sums = lax.fori_loop(0, 18 - 2 * k, row, (zero, zero))
         partial[2 * k] = sums[0]
         partial[2 * k + 1] = sums[1]
-        return later, before, now
-
-    lax.fori_loop(0, 4, operator_step, (jnp.int32(0), jnp.int32(1), jnp.int32(2)))
+        return later, 3 - now - later, now
+
+    lax.fori_loop(0, 4, operator_step, (jnp.int32(0), jnp.int32(1), jnp.int32(0)))
 
     def look(x, _):
         for c in range(3):
@@ -384,7 +439,8 @@
 def call(kernel, outs, ins, mib, scratch=(), flops=1000000):
     return pl.pallas_call(
         kernel, out_shape=outs, in_specs=[VMEM] * len(ins), out_specs=jax.tree.map(lambda _: VMEM, outs),
-        scratch_shapes=list(scratch), compiler_params=pltpu.CompilerParams(vmem_limit_bytes=int(mib * 2**20)),
+        scratch_shapes=list(scratch),
+        compiler_params=pltpu.CompilerParams(vmem_limit_bytes=mib << 20),
         cost_estimate=pl.CostEstimate(flops=flops, bytes_accessed=1 << 20, transcendentals=0))(*ins)
 
 
@@ -401,18 +457,25 @@
     c, *ends = call(load, face, (curl,), 8)
     c = (c,) + exchange(*ends, "gx")
     m, *ends = call(load_mass, face, (mass, c[0]), 8)
-    block = b + (m,) + exchange(*ends, "gx") + c
-    low, high = call(pack_y, (shape(9, 8, 8, 128),) * 2, block, 8)
-    block += exchange(low, high, "gy")
-    low, high, field, coef = call(
-        pack_z, (shape(9, ROWS, 128),) * 2 + (shape(3, X, Y, 128), shape(6, X, Y, 128)), block, 20)
-    sides = (low, high) + exchange(low, high, "gz")
+    m = (m,) + exchange(*ends, "gx")
+    ends = (shape(9, 4, 8, 128),) * 2
+    y_own = exchange(*call(pack_y_own, ends, (b[0], m[0], c[0]), 8), "gy")
+    y_halo = exchange(*call(pack_y_halo, ends, b[1:] + m[1:] + c[1:], 8), "gy")
+    columns = (shape(9, ROWS, 128),) * 2
+    extended = (shape(3, X, Y, 128), shape(6, X, Y, 128))
+    low, high, *middle = call(pack_z_middle, columns + extended, b + m + c, 8, flops=20000000)
+    low, high, *ends, field, coef = call(
+        pack_z_edge, columns + (shape(5, ROWS, 128),) * 2 + (shape(3, 16, 16, 128), shape(6, 16, 16, 128)),
+        y_own + y_halo + (low, high), 8)
+    sides = (low, high) + exchange(*ends, "gz")
+    block = call(invert, extended + (shape(3, X, Y, 128), shape(X, Y, 128)), (*middle, field, coef), 8, flops=20000000)
 
     def held(*dims):
         return pltpu.VMEM(dims + (Y, 128), jnp.float32)
 
     vectors, precond, partial, _ = call(
-        main, (shape(4, 3, 9, 32, 128), shape(4, 3, 9, 32, 128), shape(8, 8, 128), shape(2, 4, 8, 128)), (field, coef) + sides, 40,
+        main, (shape(4, 3, 9, 32, 128), shape(4, 3, 9, 32, 128), shape(8, 8, 128), shape(2, 4, 8, 128)),
+        tuple(block) + sides, 24,
         [held(3, 3, X), held(3, X), held(X), held(3, X), held(X), held(3, X),
          held(3, 3, 2), held(6, 2), held(3, 2), held(2), held(3, 2), held(2), held(3, 2)])
     axes = ("gx", "gy", "gz")

time: 75.7 us -> 68.9 us (0.910)
  waiting for transfers between devices: 14.4 us -> 2.9 us
  starting transfers between devices: 16.4 us -> 20.7 us
  Pallas kernels: 22.7 us -> 23.8 us
  blocking collectives: 18.3 us -> 17.5 us
    ppermute x5 -> x6, waiting for transfers between devices: 10 us -> 0.16 us  [exchange(): lax.ppermute(high, axis, up)]
    ppermute x5 -> x6, starting transfers between devices: 5.27 us -> 9.17 us  [exchange(): lax.ppermute(high, axis, up)]
    ppermute x5 -> x6, waiting for transfers between devices: 4.33 us -> 2.74 us  [exchange(): lax.ppermute(low, axis, [(j, i) for i, j in up])]
    pallas_call x8 -> x11, Pallas kernels: 22.7 us -> 23.8 us  [call(): pl.pallas_call(kernel, out_shape=outs, in_specs=[VMEM] * len(ins), out_sp...]
    all_to_all x1, blocking collectives: 18.3 us -> 17.5 us  [body(): lax.all_to_all(rows.reshape(devices, 1, 128), axes, 0, 0, tiled=True)]
    ppermute x5 -> x6, starting transfers between devices: 11.2 us -> 11.5 us  [exchange(): lax.ppermute(low, axis, [(j, i) for i, j in up])]
  transfers between devices with their start and end apart: 10 -> 12, of which waited for: 6 -> 3; matrix products, arithmetic and copies ran while one was open for 0% -> 0% of each run, Pallas kernels for 0% -> 9%
where the time goes in v2:
time: 68.9 us; the launch traced here: 68.6 us
  Pallas kernels  23.8 us (35%)
  starting transfers between devices  20.7 us (30%)
  blocking collectives  17.5 us (25%)
  local copies, waits for them, and re-layouts  2.98 us (4%)
  waiting for transfers between devices  2.9 us (4%)
  between operations  0.76 us (1%)
    pallas_call x11, Pallas kernels, call(): pl.pallas_call(kernel, out_shape=outs, in_specs=[VMEM] * len(ins), out_sp...  23.8 us
    all_to_all x1, blocking collectives, body(): lax.all_to_all(rows.reshape(devices, 1, 128), axes, 0, 0, tiled=True)  17.5 us
    ppermute x6, starting transfers between devices, exchange(): lax.ppermute(low, axis, [(j, i) for i, j in up])  11.5 us
    ppermute x6, starting transfers between devices, exchange(): lax.ppermute(high, axis, up)  9.17 us
    unnamed x6, local copies, waits for them, and re-layouts  2.98 us
    ppermute x6, waiting for transfers between devices, exchange(): lax.ppermute(low, axis, [(j, i) for i, j in up])  2.74 us
  transfers between devices with their start and end apart: 12, of which 3 were waited for; matrix products, arithmetic and copies ran while one was open for 0% of the time, Pallas kernels for 9%

profile of v2, /device:TPU:1, one launch (start us, length us, event | category | flops | bytes accessed | tf_op | source)
XLA Modules:
  0.0 68.6 jit_solution(14694962665152876687)
XLA Ops:
  0.6 1.0 %copy-done = f32[3,8,32,128]{3,2,1,0:T(8,128)S(1)} copy-done((f32[3,8,32,128]{3,2,1,0:T(8,128)S(1)}, f32[3,8,32,128]{3,2,1,0:T(8,128)}, u32[]{:S(2)}) %copy-start) | copy-done | bytes 393240
  1.7 2.1 %collective-permute-start = (f32[3,4,32,128]{3,2,1,0:T(8,128)S(1)}, f32[3,4,32,128]{3,2,1,0:T(8,128)S(1)}, u32[]{:S(2)}, u32[]{:S(2)}) collective-permute-start(f32[3,4,32,128]{3,2,1,0:T(8,128)S(1)} %get-tuple-element.33), channel_id=1, source_target_pairs={{0,32},{32,64},{64,96},{96,0},{1,33},{33,65},{65,97},{97,1},{2,34}... | collective-permute-start | bytes 589832 | tf_op jit(solution)/shard_map/ppermute | solution.py:450
  3.8 1.3 %collective-permute-start.1 = (f32[3,4,32,128]{3,2,1,0:T(8,128)S(1)}, f32[3,4,32,128]{3,2,1,0:T(8,128)S(1)}, u32[]{:S(2)}, u32[]{:S(2)}) collective-permute-start(f32[3,4,32,128]{3,2,1,0:T(8,128)S(1)} %get-tuple-element.34), channel_id=1, source_target_pairs={{32,0},{64,32},{96,64},{0,96},{33,1},{65,33},{97,65},{1,97},{34,2}... | collective-permute-start | bytes 589832 | tf_op jit(solution)/shard_map/ppermute | solution.py:450
  5.1 1.0 %copy-done.1 = f32[3,8,32,128]{3,2,1,0:T(8,128)S(1)} copy-done((f32[3,8,32,128]{3,2,1,0:T(8,128)S(1)}, f32[3,8,32,128]{3,2,1,0:T(8,128)}, u32[]{:S(2)}) %copy-start.1) | copy-done | bytes 393240
  6.2 0.2 collective-permute-start.4
  6.4 2.6 %collective-permute-start.5 = (f32[3,4,32,128]{3,2,1,0:T(8,128)S(1)}, f32[3,4,32,128]{3,2,1,0:T(8,128)S(1)}, u32[]{:S(2)}, u32[]{:S(2)}) collective-permute-start(f32[3,4,32,128]{3,2,1,0:T(8,128)S(1)} %get-tuple-element.40), channel_id=1, source_target_pairs={{32,0},{64,32},{96,64},{0,96},{33,1},{65,33},{97,65},{1,97},{34,2}... | collective-permute-start | bytes 589832 | tf_op jit(solution)/shard_map/ppermute | solution.py:450
  8.9 1.0 %copy-done.2 = f32[3,8,32,128]{3,2,1,0:T(8,128)S(1)} copy-done((f32[3,8,32,128]{3,2,1,0:T(8,128)S(1)}, f32[3,8,32,128]{3,2,1,0:T(8,128)}, u32[]{:S(2)}) %copy-start.2) | copy-done | bytes 393240
  10.0 0.1 collective-permute-start.2
  10.1 2.7 %collective-permute-start.3 = (f32[3,4,32,128]{3,2,1,0:T(8,128)S(1)}, f32[3,4,32,128]{3,2,1,0:T(8,128)S(1)}, u32[]{:S(2)}, u32[]{:S(2)}) collective-permute-start(f32[3,4,32,128]{3,2,1,0:T(8,128)S(1)} %get-tuple-element.38), channel_id=1, source_target_pairs={{32,0},{64,32},{96,64},{0,96},{33,1},{65,33},{97,65},{1,97},{34,2}... | collective-permute-start | bytes 589832 | tf_op jit(solution)/shard_map/ppermute | solution.py:450
  12.8 1.8 %collective-permute-start.6 = (f32[9,4,8,128]{3,2,1,0:T(8,128)S(1)}, f32[9,4,8,128]{3,2,1,0:T(8,128)S(1)}, u32[]{:S(2)}, u32[]{:S(2)}) collective-permute-start(f32[9,4,8,128]{3,2,1,0:T(8,128)S(1)} %get-tuple-element.43), channel_id=1, source_target_pairs={{0,8},{8,16},{16,24},{24,0},{1,9},{9,17},{17,25},{25,1},{2,10},{10... | collective-permute-start | bytes 442376 | tf_op jit(solution)/shard_map/ppermute | solution.py:450
  14.7 2.7 %collective-permute-start.7 = (f32[9,4,8,128]{3,2,1,0:T(8,128)S(1)}, f32[9,4,8,128]{3,2,1,0:T(8,128)S(1)}, u32[]{:S(2)}, u32[]{:S(2)}) collective-permute-start(f32[9,4,8,128]{3,2,1,0:T(8,128)S(1)} %get-tuple-element.44), channel_id=1, source_target_pairs={{8,0},{16,8},{24,16},{0,24},{9,1},{17,9},{25,17},{1,25},{10,2},{18... | collective-permute-start | bytes 442376 | tf_op jit(solution)/shard_map/ppermute | solution.py:450
  17.4 0.3 collective-permute-done.3.refs_5_.refs_3_
  17.8 1.7 %collective-permute-start.8 = (f32[9,4,8,128]{3,2,1,0:T(8,128)S(1)}, f32[9,4,8,128]{3,2,1,0:T(8,128)S(1)}, u32[]{:S(2)}, u32[]{:S(2)}) collective-permute-start(f32[9,4,8,128]{3,2,1,0:T(8,128)S(1)} %get-tuple-element.45), channel_id=1, source_target_pairs={{0,8},{8,16},{16,24},{24,0},{1,9},{9,17},{17,25},{25,1},{2,10},{10... | collective-permute-start | bytes 442376 | tf_op jit(solution)/shard_map/ppermute | solution.py:450
  19.5 2.2 %collective-permute-start.9 = (f32[9,4,8,128]{3,2,1,0:T(8,128)S(1)}, f32[9,4,8,128]{3,2,1,0:T(8,128)S(1)}, u32[]{:S(2)}, u32[]{:S(2)}) collective-permute-start(f32[9,4,8,128]{3,2,1,0:T(8,128)S(1)} %get-tuple-element.46), channel_id=1, source_target_pairs={{8,0},{16,8},{24,16},{0,24},{9,1},{17,9},{25,17},{1,25},{10,2},{18... | collective-permute-start | bytes 442376 | tf_op jit(solution)/shard_map/ppermute | solution.py:450
  21.7 4.0 %shard_map.53 = (f32[9,48,128]{2,1,0:T(8,128)S(1)}, f32[9,48,128]{2,1,0:T(8,128)S(1)}, f32[3,24,64,128]{3,2,1,0:T(8,128)S(1)}, f32[6,24,64,128]{3,2,1,0:T(8,128)S(1)}) custom-call(f32[3,8,32,128]{3,2,1,0:T(8,128)S(1)} %get-tuple-element.32.refs_0_.own, f32[3,4,32,128]{3,2,1,0:T(8,128)S(1)} %collective-permute-done.refs_1_.refs_0_, ...), custom_call_target="tpu_custom_call" | custom-call | flops 20000000 | bytes 1048576 | tf_op jit(solution)/shard_map/pallas_call | solution.py:440
  25.7 2.1 %shard_map.56 = (f32[9,48,128]{2,1,0:T(8,128)S(1)}, f32[9,48,128]{2,1,0:T(8,128)S(1)}, f32[5,48,128]{2,1,0:T(8,128)S(1)}, f32[5,48,128]{2,1,0:T(8,128)S(1)}, f32...) custom-call(f32[9,4,8,128]{3,2,1,0:T(8,128)S(1)} %collective-permute-done.6.own_low, ...), custom_call_target="tpu_custom_call" | custom-call | flops 1000000 | bytes 1048576 | tf_op jit(solution)/shard_map/pallas_call | solution.py:440
  27.9 3.3 %collective-permute-start.10 = (f32[5,48,128]{2,1,0:T(8,128)S(1)}, f32[5,48,128]{2,1,0:T(8,128)S(1)}, u32[]{:S(2)}, u32[]{:S(2)}) collective-permute-start(f32[5,48,128]{2,1,0:T(8,128)S(1)} %get-tuple-element.57), channel_id=1, source_target_pairs={{0,1},{1,2},{2,3},{3,4},{4,5},{5,6},{6,7},{7,0},{8,9},{9,10},{10,1... | collective-permute-start | bytes 368648 | tf_op jit(solution)/shard_map/ppermute | solution.py:450
  31.1 1.7 %shard_map.57 = (f32[3,24,64,128]{3,2,1,0:T(8,128)S(1)}, f32[6,24,64,128]{3,2,1,0:T(8,128)S(1)}, f32[3,24,64,128]{3,2,1,0:T(8,128)S(1)}, f32[24,64,128]{2,1,0:T(8,128)S(1)}) custom-call(f32[3,24,64,128]{3,2,1,0:T(8,128)S(1)} %get-tuple-element.41.field_middle, f32[6,24,64,128]{3,2,1,0:T(8,128)S(1)} %get-tuple-element.42.coef_middle, ...), custom_call_target="tpu_custom_call" | custom-call | flops 20000000 | bytes 1048576 | tf_op jit(solution)/shard_map/pallas_call | solution.py:440
  32.9 0.1 collective-permute-done.10.zlow
  33.0 2.4 %collective-permute-done.11.zhigh = f32[5,48,128]{2,1,0:T(8,128)S(1)} collective-permute-done((f32[5,48,128]{2,1,0:T(8,128)S(1)}, f32[5,48,128]{2,1,0:T(8,128)S(1)}, u32[]{:S(2)}, u32[]{:S(2)}) %collective-permute-start.11) | collective-permute-done | bytes 122912 | tf_op jit(solution)/shard_map/ppermute | solution.py:450
  35.4 14.2 %shard_map.58 = (f32[4,3,9,32,128]{4,3,2,1,0:T(8,128)S(1)}, f32[4,3,9,32,128]{4,3,2,1,0:T(8,128)S(1)}, f32[8,8,128]{2,1,0:T(8,128)S(1)}, f32[2,4,8,128]{3,2,1,0:T(8,128)}) custom-call(f32[3,24,64,128]{3,2,1,0:T(8,128)S(1)} %get-tuple-element.51.field_in, f32[6,24,64,128]{3,2,1,0:T(8,128)S(1)} %get-tuple-element.52.coef, ...), custom_call_target="tpu_custom_call" | custom-call | flops 1000000 | bytes 1048576 | tf_op jit(solution)/shard_map/pallas_call | solution.py:440
  49.6 0.2 shard_map.59
  49.8 17.5 %all_to_all.5 = f32[128,1,128]{2,1,0:T(1,128)S(1)} all-to-all(f32[128,1,128]{2,1,0:T(1,128)S(1)} %bitcast.5), channel_id=1, replica_groups=mesh['gx'=4,'gy'=4,'gz'=8] {'gx','gy','gz'}, dimensions={0} | all-to-all | bytes 131072 | tf_op jit(solution)/shard_map/all_to_all | solution.py:484
  67.4 1.3 %shard_map.60 = (f32[3,8,32,128]{3,2,1,0:T(8,128)}, f32[3,8,32,128]{3,2,1,0:T(8,128)}) custom-call(f32[128,128]{1,0:T(8,128)S(1)} %bitcast.4, f32[3,8,32,128]{3,2,1,0:T(8,128)S(1)} %get-tuple-element.32.refs_0_.own, f32[4,3,9,32,128]{4,3,2,1,0:T(8,128)S(1)} %get-tuple-element.60.vectors, f32[4,3,9,32,128]{4,3,2,1,0:T(8,128)S(1)} %get-tuple-element.61.precond), custom_call_target="tpu_custom_call" | custom-call | flops 1000000 | bytes 1048576 | tf_op jit(solution)/shard_map/pallas_call | solution.py:440
  (18 shorter events, 0.3 us)
Async XLA Ops:
  0.6 1.0 %copy-start = (f32[3,8,32,128]{3,2,1,0:T(8,128)S(1)}, f32[3,8,32,128]{3,2,1,0:T(8,128)}, u32[]{:S(2)}) copy-start(f32[3,8,32,128]{3,2,1,0:T(8,128)} %source.3) | copy-start | bytes 1179652
  1.7 8.4 %collective-permute-start = (f32[3,4,32,128]{3,2,1,0:T(8,128)S(1)}, f32[3,4,32,128]{3,2,1,0:T(8,128)S(1)}, u32[]{:S(2)}, u32[]{:S(2)}) collective-permute-start(f32[3,4,32,128]{3,2,1,0:T(8,128)S(1)} %get-tuple-element.33), channel_id=1, source_target_pairs={{0,32},{32,64},{64,96},{96,0},{1,33},{33,65},{65,97},{97,1},{2,34}... | collective-permute-start | bytes 589832 | tf_op jit(solution)/shard_map/ppermute | solution.py:450
  3.8 9.0 %collective-permute-start.1 = (f32[3,4,32,128]{3,2,1,0:T(8,128)S(1)}, f32[3,4,32,128]{3,2,1,0:T(8,128)S(1)}, u32[]{:S(2)}, u32[]{:S(2)}) collective-permute-start(f32[3,4,32,128]{3,2,1,0:T(8,128)S(1)} %get-tuple-element.34), channel_id=1, source_target_pairs={{32,0},{64,32},{96,64},{0,96},{33,1},{65,33},{97,65},{1,97},{34,2}... | collective-permute-start | bytes 589832 | tf_op jit(solution)/shard_map/ppermute | solution.py:450
  5.1 1.0 %copy-start.1 = (f32[3,8,32,128]{3,2,1,0:T(8,128)S(1)}, f32[3,8,32,128]{3,2,1,0:T(8,128)}, u32[]{:S(2)}) copy-start(f32[3,8,32,128]{3,2,1,0:T(8,128)} %source.4) | copy-start | bytes 1179652
  6.2 8.5 %collective-permute-start.4 = (f32[3,4,32,128]{3,2,1,0:T(8,128)S(1)}, f32[3,4,32,128]{3,2,1,0:T(8,128)S(1)}, u32[]{:S(2)}, u32[]{:S(2)}) collective-permute-start(f32[3,4,32,128]{3,2,1,0:T(8,128)S(1)} %get-tuple-element.39), channel_id=1, source_target_pairs={{0,32},{32,64},{64,96},{96,0},{1,33},{33,65},{65,97},{97,1},{2,34}... | collective-permute-start | bytes 589832 | tf_op jit(solution)/shard_map/ppermute | solution.py:450
  6.4 11.0 %collective-permute-start.5 = (f32[3,4,32,128]{3,2,1,0:T(8,128)S(1)}, f32[3,4,32,128]{3,2,1,0:T(8,128)S(1)}, u32[]{:S(2)}, u32[]{:S(2)}) collective-permute-start(f32[3,4,32,128]{3,2,1,0:T(8,128)S(1)} %get-tuple-element.40), channel_id=1, source_target_pairs={{32,0},{64,32},{96,64},{0,96},{33,1},{65,33},{97,65},{1,97},{34,2}... | collective-permute-start | bytes 589832 | tf_op jit(solution)/shard_map/ppermute | solution.py:450
  8.9 1.0 %copy-start.2 = (f32[3,8,32,128]{3,2,1,0:T(8,128)S(1)}, f32[3,8,32,128]{3,2,1,0:T(8,128)}, u32[]{:S(2)}) copy-start(f32[3,8,32,128]{3,2,1,0:T(8,128)} %source.5) | copy-start | bytes 1179652
  10.0 7.4 %collective-permute-start.2 = (f32[3,4,32,128]{3,2,1,0:T(8,128)S(1)}, f32[3,4,32,128]{3,2,1,0:T(8,128)S(1)}, u32[]{:S(2)}, u32[]{:S(2)}) collective-permute-start(f32[3,4,32,128]{3,2,1,0:T(8,128)S(1)} %get-tuple-element.37), channel_id=1, source_target_pairs={{0,32},{32,64},{64,96},{96,0},{1,33},{33,65},{65,97},{97,1},{2,34}... | collective-permute-start | bytes 589832 | tf_op jit(solution)/shard_map/ppermute | solution.py:450
  10.1 7.6 %collective-permute-start.3 = (f32[3,4,32,128]{3,2,1,0:T(8,128)S(1)}, f32[3,4,32,128]{3,2,1,0:T(8,128)S(1)}, u32[]{:S(2)}, u32[]{:S(2)}) collective-permute-start(f32[3,4,32,128]{3,2,1,0:T(8,128)S(1)} %get-tuple-element.38), channel_id=1, source_target_pairs={{32,0},{64,32},{96,64},{0,96},{33,1},{65,33},{97,65},{1,97},{34,2}... | collective-permute-start | bytes 589832 | tf_op jit(solution)/shard_map/ppermute | solution.py:450
  12.8 12.9 %collective-permute-start.6 = (f32[9,4,8,128]{3,2,1,0:T(8,128)S(1)}, f32[9,4,8,128]{3,2,1,0:T(8,128)S(1)}, u32[]{:S(2)}, u32[]{:S(2)}) collective-permute-start(f32[9,4,8,128]{3,2,1,0:T(8,128)S(1)} %get-tuple-element.43), channel_id=1, source_target_pairs={{0,8},{8,16},{16,24},{24,0},{1,9},{9,17},{17,25},{25,1},{2,10},{10... | collective-permute-start | bytes 442376 | tf_op jit(solution)/shard_map/ppermute | solution.py:450
  14.7 11.1 %collective-permute-start.7 = (f32[9,4,8,128]{3,2,1,0:T(8,128)S(1)}, f32[9,4,8,128]{3,2,1,0:T(8,128)S(1)}, u32[]{:S(2)}, u32[]{:S(2)}) collective-permute-start(f32[9,4,8,128]{3,2,1,0:T(8,128)S(1)} %get-tuple-element.44), channel_id=1, source_target_pairs={{8,0},{16,8},{24,16},{0,24},{9,1},{17,9},{25,17},{1,25},{10,2},{18... | collective-permute-start | bytes 442376 | tf_op jit(solution)/shard_map/ppermute | solution.py:450
  17.8 7.9 %collective-permute-start.8 = (f32[9,4,8,128]{3,2,1,0:T(8,128)S(1)}, f32[9,4,8,128]{3,2,1,0:T(8,128)S(1)}, u32[]{:S(2)}, u32[]{:S(2)}) collective-permute-start(f32[9,4,8,128]{3,2,1,0:T(8,128)S(1)} %get-tuple-element.45), channel_id=1, source_target_pairs={{0,8},{8,16},{16,24},{24,0},{1,9},{9,17},{17,25},{25,1},{2,10},{10... | collective-permute-start | bytes 442376 | tf_op jit(solution)/shard_map/ppermute | solution.py:450
  19.5 6.2 %collective-permute-start.9 = (f32[9,4,8,128]{3,2,1,0:T(8,128)S(1)}, f32[9,4,8,128]{3,2,1,0:T(8,128)S(1)}, u32[]{:S(2)}, u32[]{:S(2)}) collective-permute-start(f32[9,4,8,128]{3,2,1,0:T(8,128)S(1)} %get-tuple-element.46), channel_id=1, source_target_pairs={{8,0},{16,8},{24,16},{0,24},{9,1},{17,9},{25,17},{1,25},{10,2},{18... | collective-permute-start | bytes 442376 | tf_op jit(solution)/shard_map/ppermute | solution.py:450
  27.9 5.2 %collective-permute-start.10 = (f32[5,48,128]{2,1,0:T(8,128)S(1)}, f32[5,48,128]{2,1,0:T(8,128)S(1)}, u32[]{:S(2)}, u32[]{:S(2)}) collective-permute-start(f32[5,48,128]{2,1,0:T(8,128)S(1)} %get-tuple-element.57), channel_id=1, source_target_pairs={{0,1},{1,2},{2,3},{3,4},{4,5},{5,6},{6,7},{7,0},{8,9},{9,10},{10,1... | collective-permute-start | bytes 368648 | tf_op jit(solution)/shard_map/ppermute | solution.py:450
  31.1 4.3 %collective-permute-start.11 = (f32[5,48,128]{2,1,0:T(8,128)S(1)}, f32[5,48,128]{2,1,0:T(8,128)S(1)}, u32[]{:S(2)}, u32[]{:S(2)}) collective-permute-start(f32[5,48,128]{2,1,0:T(8,128)S(1)} %get-tuple-element.58), channel_id=1, source_target_pairs={{1,0},{2,1},{3,2},{4,3},{5,4},{6,5},{7,6},{0,7},{9,8},{10,9},{11,1... | collective-permute-start | bytes 368648 | tf_op jit(solution)/shard_map/ppermute | solution.py:450

commit v3 on v2

--- a/solution.py
+++ b/solution.py
@@ -6,9 +6,9 @@
 from jax.sharding import PartitionSpec as P
 
 
-X, Y = 24, 64
-OFF, OWN = 4, 16
-LO, ROWS = 8, 48
+X, Y = 24, 56
+OFF, OWN = 4, 12
+LO, ROWS = 8, 40
 WEIGHT = (0.0, 0.5, 0.25, 0.25, 0.25)
 VMEM = pl.BlockSpec(memory_space=pltpu.VMEM)
 
@@ -120,31 +120,32 @@
         return 0
 
     lax.fori_loop(0, 3, assemble, 0)
-    all_strips(field, coef, (4, OFF, OWN, 8, 8), low, high)
-
-
-def pack_z_edge(own_low, own_high, halo_low, halo_high, middle_low, middle_high,
+    all_strips(field, coef, (3, OFF, 16, 8, 8), low, high)
+
+
+def pack_z_edge(own_low, own_high, halo_low, halo_high, middle_low, middle_high, middle_field, middle_coef,
                 low, high, send_low, send_high, field, coef):
     sub = lax.broadcasted_iota(jnp.int32, (8, 128), 0)
 
     def assemble(c, _):
         for n in range(3):
             to = field.at[c] if n == 0 else coef.at[3 * n - 3 + c]
+            source = middle_field.at[c] if n == 0 else middle_coef.at[3 * n - 3 + c]
             comp = 3 * n + c
             for p in range(4):
                 for lows, highs, x0, x1 in ((halo_low, halo_high, p, p + 12), (own_low, own_high, p + 4, p + 8)):
                     lower, upper = lows[comp, p], highs[comp, p]
-                    to[x0, 0:8] = jnp.where(sub >= 4, pltpu.roll(lower, 4, 0), 0.0)
-                    to[x1, 0:8] = jnp.where(sub >= 4, lower, 0.0)
-                    to[x0, 8:16] = jnp.where(sub < 4, upper, 0.0)
-                    to[x1, 8:16] = jnp.where(sub < 4, pltpu.roll(upper, 4, 0), 0.0)
+                    to[x0, 0:8] = jnp.where(sub < 4, lower, source[OFF + x0, 8:16])
+                    to[x1, 0:8] = jnp.where(sub < 4, pltpu.roll(lower, 4, 0), source[OFF + x1, 8:16])
+                    to[x0, 8:16] = jnp.where(sub < 4, source[OFF + x0, 40:48], pltpu.roll(upper, 4, 0))
+                    to[x1, 8:16] = jnp.where(sub < 4, source[OFF + x1, 40:48], upper)
         return 0
 
     lax.fori_loop(0, 3, assemble, 0)
-    all_strips(field, coef, (2, 0, 0, 0, 40), low, high)
+    all_strips(field, coef, (2, 0, 0, 0, 32), low, high)
     for comp in range(9):
-        low[comp, 8:40] = middle_low[comp, 8:40]
-        high[comp, 8:40] = middle_high[comp, 8:40]
+        low[comp, 8:32] = middle_low[comp, 8:32]
+        high[comp, 8:32] = middle_high[comp, 8:32]
     for n in range(5):
         down, up = low[n], high[n]
         if n < 4:
@@ -173,16 +174,17 @@
     def assemble(c, _):
         coef[c, OFF - 1] = jnp.zeros((Y, 128), jnp.float32)
         for x in range(OFF, OFF + 16):
-            coef[c, x, OWN : OWN + 32] = coef_middle[c, x, OWN : OWN + 32]
-            coef[c, x, OWN - 8 : OWN] = coef_edge[c, x - OFF, 0:8]
-            coef[c, x, OWN + 32 : OWN + 40] = coef_edge[c, x - OFF, 8:16]
+            coef[c, x, 0:8] = jnp.zeros((8, 128), jnp.float32)
+            coef[c, x, 16:40] = coef_middle[c, x, 16:40]
+            coef[c, x, 8:16] = coef_edge[c, x - OFF, 0:8]
+            coef[c, x, 40:48] = coef_edge[c, x - OFF, 8:16]
         return 0
 
     def assemble_field(c, _):
         for x in range(OFF, OFF + 16):
-            field[c, x, OWN : OWN + 32] = field_middle[c, x, OWN : OWN + 32]
-            field[c, x, OWN - 8 : OWN] = field_edge[c, x - OFF, 0:8]
-            field[c, x, OWN + 32 : OWN + 40] = field_edge[c, x - OFF, 8:16]
+            field[c, x, 16:40] = field_middle[c, x, 16:40]
+            field[c, x, 8:16] = field_edge[c, x - OFF, 0:8]
+            field[c, x, 40:48] = field_edge[c, x - OFF, 8:16]
         return 0
 
     lax.fori_loop(0, 6, assemble, 0)
@@ -204,11 +206,12 @@
     lax.fori_loop(0, 16, row, 0)
 
 
-def main(field_in, coef, diag_in, node_in, zown_low, zown_high, zlow, zhigh, vectors, precond, partial, sink,
-         field, diag, node, s, phi, g, fieldS, coefS, diagS, nodeS, sS, phiS, gS):
+def main(field_in, coef, diag_in, node_in, zown_low, zown_high, zlow, zhigh, field, precond, partial, sink,
+         diag, node, s, phi, g, fieldS, coefS, diagS, nodeS, sS, phiS, gS):
     f32 = jnp.float32
     lane = lax.broadcasted_iota(jnp.int32, (ROWS, 128), 1)
     first_lane, last_lane = lane == 0, lane == 127
+    below_half = lax.broadcasted_iota(jnp.int32, (8, 128), 0) < 4
 
     def z_up(value, strip, x):
         return jnp.where(last_lane, pltpu.roll(strip, (123 - 8 * x) & 127, 1), pltpu.roll(value, 127, 1))
@@ -224,6 +227,8 @@
         for t, value in ((0, jnp.where(upper, zown_low[comp], lower_part)),
                          (1, jnp.where(upper, upper_part, zown_high[comp]))):
             put(fieldS.at[0, comp, t] if comp < 3 else coefS.at[comp - 3, t], value)
+            if comp >= 3:
+                coefS[comp - 3, t, 0:8] = jnp.zeros((8, 128), f32)
 
     def setup_strip(t, _):
         m = [at(coefS.at[c, t]) for c in range(3)]
@@ -257,8 +262,8 @@
     def curl_back(gv, g0y, g0z, g1x, g1z, g2x, g2y):
         return ((g1z - gv[1]) - (g2y - gv[2]), (g2x - gv[2]) - (g0z - gv[0]), (g0y - gv[0]) - (g1x - gv[1]))
 
-    def operator_step(k, turns):
-        now, later, before = turns
+    def operator_step(k, _):
+        now, later, before = k, k + 1, jnp.maximum(k - 1, 0)
         weight = jnp.where(k == 0, 0.0, jnp.where(k == 1, 0.5, 0.25))
 
         def strip_first(t, _):
@@ -334,11 +339,10 @@
             put(phi.at[b], potential)
             sums = list(sums)
             for c in range(3):
-                uo, ro, vo = (z[OWN - LO : OWN - LO + 32] for z in (u[c], r[c], v[c]))
-                vectors[k, c, to] = vo
-                precond[k, c, to] = uo
-                for n, prod in ((0, ro * uo), (1, vo * uo)):
-                    part = (prod[0:8] + prod[8:16]) + (prod[16:24] + prod[24:32])
+                precond[k, c, to] = u[c]
+                for n, prod in ((0, r[c] * u[c]), (1, v[c] * u[c])):
+                    ends = jnp.where(below_half, prod[32:40], prod[0:8])
+                    part = ((prod[8:16] + prod[16:24]) + prod[24:32]) + ends
                     sums[n] = sums[n] + jnp.where(inside, part, 0.0)
             return tuple(sums)
 
@@ -346,9 +350,9 @@
         sums = lax.fori_loop(0, 18 - 2 * k, row, (zero, zero))
         partial[2 * k] = sums[0]
         partial[2 * k + 1] = sums[1]
-        return later, 3 - now - later, now
-
-    lax.fori_loop(0, 4, operator_step, (jnp.int32(0), jnp.int32(1), jnp.int32(0)))
+        return 0
+
+    lax.fori_loop(0, 4, operator_step, 0)
 
     def look(x, _):
         for c in range(3):
@@ -370,7 +374,7 @@
     out[...] = jnp.broadcast_to(row, out.shape)
 
 
-def finish(everyone, own, vectors, precond, solution_out, residual_out):
+def finish(everyone, field, precond, solution_out, residual_out):
     total = jnp.sum(everyone[...], axis=0, keepdims=True)
     lane = lax.broadcasted_iota(jnp.int32, (1, 128), 1)
     dots = [jnp.broadcast_to(jnp.sum(jnp.where(lane // 16 == d, total, 0.0), axis=1, keepdims=True), (8, 128))
@@ -422,11 +426,12 @@
     S = [v[0:1] for v in S]
 
     def combine(x, _):
+        rows, first = pl.ds(OWN, 32), pl.ds(OWN - LO, 32)
         for c in range(3):
-            residual_out[c, x] = (e[0] * own[c, x] + e[1] * vectors[0, c, x]) + (
-                e[2] * vectors[1, c, x] + e[3] * vectors[2, c, x]) + e[4] * vectors[3, c, x]
-            solution_out[c, x] = (S[0] * precond[0, c, x] + S[1] * precond[1, c, x]) + (
-                S[2] * precond[2, c, x] + S[3] * precond[3, c, x])
+            v = [field[k, c, x + OFF + 4, rows, :] for k in range(5)]
+            u = [precond[k, c, x, first, :] for k in range(4)]
+            residual_out[c, x] = (e[0] * v[0] + e[1] * v[1]) + (e[2] * v[2] + e[3] * v[3]) + e[4] * v[4]
+            solution_out[c, x] = (S[0] * u[0] + S[1] * u[1]) + (S[2] * u[2] + S[3] * u[3])
         return 0
 
     lax.fori_loop(0, 8, combine, 0)
@@ -466,7 +471,7 @@
     low, high, *middle = call(pack_z_middle, columns + extended, b + m + c, 8, flops=20000000)
     low, high, *ends, field, coef = call(
         pack_z_edge, columns + (shape(5, ROWS, 128),) * 2 + (shape(3, 16, 16, 128), shape(6, 16, 16, 128)),
-        y_own + y_halo + (low, high), 8)
+        y_own + y_halo + (low, high, *middle), 8)
     sides = (low, high) + exchange(*ends, "gz")
     block = call(invert, extended + (shape(3, X, Y, 128), shape(X, Y, 128)), (*middle, field, coef), 8, flops=20000000)
 
@@ -474,15 +479,15 @@
         return pltpu.VMEM(dims + (Y, 128), jnp.float32)
 
     vectors, precond, partial, _ = call(
-        main, (shape(4, 3, 9, 32, 128), shape(4, 3, 9, 32, 128), shape(8, 8, 128), shape(2, 4, 8, 128)),
-        tuple(block) + sides, 24,
-        [held(3, 3, X), held(3, X), held(X), held(3, X), held(X), held(3, X),
-         held(3, 3, 2), held(6, 2), held(3, 2), held(2), held(3, 2), held(2), held(3, 2)])
+        main, (shape(5, 3, X, Y, 128), shape(4, 3, 9, ROWS, 128), shape(8, 8, 128), shape(2, 4, 8, 128)),
+        tuple(block) + sides, 20,
+        [held(3, X), held(X), held(3, X), held(X), held(3, X),
+         held(5, 3, 2), held(6, 2), held(3, 2), held(2), held(3, 2), held(2), held(3, 2)])
     axes = ("gx", "gy", "gz")
     devices = lax.axis_size(axes)
     (rows,) = call(fold, (shape(devices, 128),), (partial,), 4)
     everyone = lax.all_to_all(rows.reshape(devices, 1, 128), axes, 0, 0, tiled=True).reshape(devices, 128)
-    return call(finish, (shape(3, 8, 32, 128),) * 2, (everyone, b[0], vectors, precond), 16)
+    return call(finish, (shape(3, 8, 32, 128),) * 2, (everyone, vectors, precond), 16)
 
 
 def solution(mesh):

time: 68.9 us -> 67.5 us (0.980)
  Pallas kernels: 23.8 us -> 21.7 us
  blocking collectives: 17.5 us -> 18.4 us
    pallas_call x11, Pallas kernels: 23.8 us -> 21.7 us  [call(): pl.pallas_call(kernel, out_shape=outs, in_specs=[VMEM] * len(ins), out_sp...]
    all_to_all x1, blocking collectives: 17.5 us -> 18.4 us  [body(): lax.all_to_all(rows.reshape(devices, 1, 128), axes, 0, 0, tiled=True)]
  transfers between devices with their start and end apart: 12 -> 12, of which waited for: 3 -> 2; matrix products, arithmetic and copies ran while one was open for 0% -> 0% of each run, Pallas kernels for 9% -> 8%
where the time goes in v3:
time: 67.5 us; the launch traced here: 67.3 us
  Pallas kernels  21.7 us (32%)
  starting transfers between devices  20.7 us (31%)
  blocking collectives  18.4 us (27%)
  local copies, waits for them, and re-layouts  2.98 us (4%)
  waiting for transfers between devices  2.73 us (4%)
  between operations  0.77 us (1%)
    pallas_call x11, Pallas kernels, call(): pl.pallas_call(kernel, out_shape=outs, in_specs=[VMEM] * len(ins), out_sp...  21.7 us
    all_to_all x1, blocking collectives, body(): lax.all_to_all(rows.reshape(devices, 1, 128), axes, 0, 0, tiled=True)  18.4 us
    ppermute x6, starting transfers between devices, exchange(): lax.ppermute(low, axis, [(j, i) for i, j in up])  11.5 us
    ppermute x6, starting transfers between devices, exchange(): lax.ppermute(high, axis, up)  9.17 us
    unnamed x6, local copies, waits for them, and re-layouts  2.98 us
    ppermute x6, waiting for transfers between devices, exchange(): lax.ppermute(low, axis, [(j, i) for i, j in up])  2.69 us
  transfers between devices with their start and end apart: 12, of which 2 were waited for; matrix products, arithmetic and copies ran while one was open for 0% of the time, Pallas kernels for 8%

profile of v3, /device:TPU:1, one launch (start us, length us, event | category | flops | bytes accessed | tf_op | source)
XLA Modules:
  0.0 67.3 jit_solution(4530772723097589163)
XLA Ops:
  0.6 1.0 %copy-done = f32[3,8,32,128]{3,2,1,0:T(8,128)S(1)} copy-done((f32[3,8,32,128]{3,2,1,0:T(8,128)S(1)}, f32[3,8,32,128]{3,2,1,0:T(8,128)}, u32[]{:S(2)}) %copy-start) | copy-done | bytes 393240
  1.7 2.1 %collective-permute-start = (f32[3,4,32,128]{3,2,1,0:T(8,128)S(1)}, f32[3,4,32,128]{3,2,1,0:T(8,128)S(1)}, u32[]{:S(2)}, u32[]{:S(2)}) collective-permute-start(f32[3,4,32,128]{3,2,1,0:T(8,128)S(1)} %get-tuple-element.33), channel_id=1, source_target_pairs={{0,32},{32,64},{64,96},{96,0},{1,33},{33,65},{65,97},{97,1},{2,34}... | collective-permute-start | bytes 589832 | tf_op jit(solution)/shard_map/ppermute | solution.py:455
  3.8 1.3 %collective-permute-start.1 = (f32[3,4,32,128]{3,2,1,0:T(8,128)S(1)}, f32[3,4,32,128]{3,2,1,0:T(8,128)S(1)}, u32[]{:S(2)}, u32[]{:S(2)}) collective-permute-start(f32[3,4,32,128]{3,2,1,0:T(8,128)S(1)} %get-tuple-element.34), channel_id=1, source_target_pairs={{32,0},{64,32},{96,64},{0,96},{33,1},{65,33},{97,65},{1,97},{34,2}... | collective-permute-start | bytes 589832 | tf_op jit(solution)/shard_map/ppermute | solution.py:455
  5.1 1.0 %copy-done.1 = f32[3,8,32,128]{3,2,1,0:T(8,128)S(1)} copy-done((f32[3,8,32,128]{3,2,1,0:T(8,128)S(1)}, f32[3,8,32,128]{3,2,1,0:T(8,128)}, u32[]{:S(2)}) %copy-start.1) | copy-done | bytes 393240
  6.2 0.2 collective-permute-start.4
  6.4 2.6 %collective-permute-start.5 = (f32[3,4,32,128]{3,2,1,0:T(8,128)S(1)}, f32[3,4,32,128]{3,2,1,0:T(8,128)S(1)}, u32[]{:S(2)}, u32[]{:S(2)}) collective-permute-start(f32[3,4,32,128]{3,2,1,0:T(8,128)S(1)} %get-tuple-element.40), channel_id=1, source_target_pairs={{32,0},{64,32},{96,64},{0,96},{33,1},{65,33},{97,65},{1,97},{34,2}... | collective-permute-start | bytes 589832 | tf_op jit(solution)/shard_map/ppermute | solution.py:455
  8.9 1.0 %copy-done.2 = f32[3,8,32,128]{3,2,1,0:T(8,128)S(1)} copy-done((f32[3,8,32,128]{3,2,1,0:T(8,128)S(1)}, f32[3,8,32,128]{3,2,1,0:T(8,128)}, u32[]{:S(2)}) %copy-start.2) | copy-done | bytes 393240
  10.0 0.1 collective-permute-start.2
  10.1 2.7 %collective-permute-start.3 = (f32[3,4,32,128]{3,2,1,0:T(8,128)S(1)}, f32[3,4,32,128]{3,2,1,0:T(8,128)S(1)}, u32[]{:S(2)}, u32[]{:S(2)}) collective-permute-start(f32[3,4,32,128]{3,2,1,0:T(8,128)S(1)} %get-tuple-element.38), channel_id=1, source_target_pairs={{32,0},{64,32},{96,64},{0,96},{33,1},{65,33},{97,65},{1,97},{34,2}... | collective-permute-start | bytes 589832 | tf_op jit(solution)/shard_map/ppermute | solution.py:455
  12.7 0.1 shard_map.54
  12.8 1.8 %collective-permute-start.6 = (f32[9,4,8,128]{3,2,1,0:T(8,128)S(1)}, f32[9,4,8,128]{3,2,1,0:T(8,128)S(1)}, u32[]{:S(2)}, u32[]{:S(2)}) collective-permute-start(f32[9,4,8,128]{3,2,1,0:T(8,128)S(1)} %get-tuple-element.43), channel_id=1, source_target_pairs={{0,8},{8,16},{16,24},{24,0},{1,9},{9,17},{17,25},{25,1},{2,10},{10... | collective-permute-start | bytes 442376 | tf_op jit(solution)/shard_map/ppermute | solution.py:455
  14.7 2.7 %collective-permute-start.7 = (f32[9,4,8,128]{3,2,1,0:T(8,128)S(1)}, f32[9,4,8,128]{3,2,1,0:T(8,128)S(1)}, u32[]{:S(2)}, u32[]{:S(2)}) collective-permute-start(f32[9,4,8,128]{3,2,1,0:T(8,128)S(1)} %get-tuple-element.44), channel_id=1, source_target_pairs={{8,0},{16,8},{24,16},{0,24},{9,1},{17,9},{25,17},{1,25},{10,2},{18... | collective-permute-start | bytes 442376 | tf_op jit(solution)/shard_map/ppermute | solution.py:455
  17.4 0.3 collective-permute-done.3.refs_5_.refs_3_
  17.8 1.7 %collective-permute-start.8 = (f32[9,4,8,128]{3,2,1,0:T(8,128)S(1)}, f32[9,4,8,128]{3,2,1,0:T(8,128)S(1)}, u32[]{:S(2)}, u32[]{:S(2)}) collective-permute-start(f32[9,4,8,128]{3,2,1,0:T(8,128)S(1)} %get-tuple-element.45), channel_id=1, source_target_pairs={{0,8},{8,16},{16,24},{24,0},{1,9},{9,17},{17,25},{25,1},{2,10},{10... | collective-permute-start | bytes 442376 | tf_op jit(solution)/shard_map/ppermute | solution.py:455
  19.5 2.2 %collective-permute-start.9 = (f32[9,4,8,128]{3,2,1,0:T(8,128)S(1)}, f32[9,4,8,128]{3,2,1,0:T(8,128)S(1)}, u32[]{:S(2)}, u32[]{:S(2)}) collective-permute-start(f32[9,4,8,128]{3,2,1,0:T(8,128)S(1)} %get-tuple-element.46), channel_id=1, source_target_pairs={{8,0},{16,8},{24,16},{0,24},{9,1},{17,9},{25,17},{1,25},{10,2},{18... | collective-permute-start | bytes 442376 | tf_op jit(solution)/shard_map/ppermute | solution.py:455
  21.7 3.2 %shard_map.53 = (f32[9,40,128]{2,1,0:T(8,128)S(1)}, f32[9,40,128]{2,1,0:T(8,128)S(1)}, f32[3,24,56,128]{3,2,1,0:T(8,128)S(1)}, f32[6,24,56,128]{3,2,1,0:T(8,128)S(1)}) custom-call(f32[3,8,32,128]{3,2,1,0:T(8,128)S(1)} %get-tuple-element.32.refs_0_, f32[3,4,32,128]{3,2,1,0:T(8,128)S(1)} %collective-permute-done.refs_1_.refs_0_, ...), custom_call_target="tpu_custom_call" | custom-call | flops 20000000 | bytes 1048576 | tf_op jit(solution)/shard_map/pallas_call | solution.py:445
  24.9 2.2 %shard_map.56 = (f32[9,40,128]{2,1,0:T(8,128)S(1)}, f32[9,40,128]{2,1,0:T(8,128)S(1)}, f32[5,40,128]{2,1,0:T(8,128)S(1)}, f32[5,40,128]{2,1,0:T(8,128)S(1)}, f32...) custom-call(f32[9,4,8,128]{3,2,1,0:T(8,128)S(1)} %collective-permute-done.6.own_low, ...), custom_call_target="tpu_custom_call" | custom-call | flops 1000000 | bytes 1048576 | tf_op jit(solution)/shard_map/pallas_call | solution.py:445
  27.1 3.3 %collective-permute-start.10 = (f32[5,40,128]{2,1,0:T(8,128)S(1)}, f32[5,40,128]{2,1,0:T(8,128)S(1)}, u32[]{:S(2)}, u32[]{:S(2)}) collective-permute-start(f32[5,40,128]{2,1,0:T(8,128)S(1)} %get-tuple-element.57), channel_id=1, source_target_pairs={{0,1},{1,2},{2,3},{3,4},{4,5},{5,6},{6,7},{7,0},{8,9},{9,10},{10,1... | collective-permute-start | bytes 307208 | tf_op jit(solution)/shard_map/ppermute | solution.py:455
  30.4 1.7 %shard_map.57 = (f32[3,24,56,128]{3,2,1,0:T(8,128)S(1)}, f32[6,24,56,128]{3,2,1,0:T(8,128)S(1)}, f32[3,24,56,128]{3,2,1,0:T(8,128)S(1)}, f32[24,56,128]{2,1,0:T(8,128)S(1)}) custom-call(f32[3,24,56,128]{3,2,1,0:T(8,128)S(1)} %get-tuple-element.41.middle_field.field_middle, f32[6,24,56,128]{3,2,1,0:T(8,128)S(1)} %get-tuple-element.42.middle_coef.coef_middle, ...), custom_call_target="tpu_custom_call" | custom-call | flops 20000000 | bytes 1048576 | tf_op jit(solution)/shard_map/pallas_call | solution.py:445
  32.1 2.4 %collective-permute-done.11.zhigh = f32[5,40,128]{2,1,0:T(8,128)S(1)} collective-permute-done((f32[5,40,128]{2,1,0:T(8,128)S(1)}, f32[5,40,128]{2,1,0:T(8,128)S(1)}, u32[]{:S(2)}, u32[]{:S(2)}) %collective-permute-start.11) | collective-permute-done | bytes 102432 | tf_op jit(solution)/shard_map/ppermute | solution.py:455
  34.4 13.0 %shard_map.58 = (f32[5,3,24,56,128]{4,3,2,1,0:T(8,128)S(1)}, f32[4,3,9,40,128]{4,3,2,1,0:T(8,128)S(1)}, f32[8,8,128]{2,1,0:T(8,128)S(1)}, f32[2,4,8,128]{3,2,1,0:T(8,128)}) custom-call(f32[3,24,56,128]{3,2,1,0:T(8,128)S(1)} %get-tuple-element.51.field_in, f32[6,24,56,128]{3,2,1,0:T(8,128)S(1)} %get-tuple-element.52.coef, ...), custom_call_target="tpu_custom_call" | custom-call | flops 1000000 | bytes 1048576 | tf_op jit(solution)/shard_map/pallas_call | solution.py:445
  47.4 0.2 shard_map.59
  47.6 18.4 %all_to_all.5 = f32[128,1,128]{2,1,0:T(1,128)S(1)} all-to-all(f32[128,1,128]{2,1,0:T(1,128)S(1)} %bitcast.5), channel_id=1, replica_groups=mesh['gx'=4,'gy'=4,'gz'=8] {'gx','gy','gz'}, dimensions={0} | all-to-all | bytes 131072 | tf_op jit(solution)/shard_map/all_to_all | solution.py:489
  66.0 1.3 %shard_map.60 = (f32[3,8,32,128]{3,2,1,0:T(8,128)}, f32[3,8,32,128]{3,2,1,0:T(8,128)}) custom-call(f32[128,128]{1,0:T(8,128)S(1)} %bitcast.4, f32[5,3,24,56,128]{4,3,2,1,0:T(8,128)S(1)} %get-tuple-element.60.field, f32[4,3,9,40,128]{4,3,2,1,0:T(8,128)S(1)} %get-tuple-element.61.precond), custom_call_target="tpu_custom_call" | custom-call | flops 1000000 | bytes 1048576 | tf_op jit(solution)/shard_map/pallas_call | solution.py:445
  (18 shorter events, 0.3 us)
Async XLA Ops:
  0.6 1.0 %copy-start = (f32[3,8,32,128]{3,2,1,0:T(8,128)S(1)}, f32[3,8,32,128]{3,2,1,0:T(8,128)}, u32[]{:S(2)}) copy-start(f32[3,8,32,128]{3,2,1,0:T(8,128)} %source.3) | copy-start | bytes 1179652
  1.7 8.4 %collective-permute-start = (f32[3,4,32,128]{3,2,1,0:T(8,128)S(1)}, f32[3,4,32,128]{3,2,1,0:T(8,128)S(1)}, u32[]{:S(2)}, u32[]{:S(2)}) collective-permute-start(f32[3,4,32,128]{3,2,1,0:T(8,128)S(1)} %get-tuple-element.33), channel_id=1, source_target_pairs={{0,32},{32,64},{64,96},{96,0},{1,33},{33,65},{65,97},{97,1},{2,34}... | collective-permute-start | bytes 589832 | tf_op jit(solution)/shard_map/ppermute | solution.py:455
  3.8 9.0 %collective-permute-start.1 = (f32[3,4,32,128]{3,2,1,0:T(8,128)S(1)}, f32[3,4,32,128]{3,2,1,0:T(8,128)S(1)}, u32[]{:S(2)}, u32[]{:S(2)}) collective-permute-start(f32[3,4,32,128]{3,2,1,0:T(8,128)S(1)} %get-tuple-element.34), channel_id=1, source_target_pairs={{32,0},{64,32},{96,64},{0,96},{33,1},{65,33},{97,65},{1,97},{34,2}... | collective-permute-start | bytes 589832 | tf_op jit(solution)/shard_map/ppermute | solution.py:455
  5.1 1.0 %copy-start.1 = (f32[3,8,32,128]{3,2,1,0:T(8,128)S(1)}, f32[3,8,32,128]{3,2,1,0:T(8,128)}, u32[]{:S(2)}) copy-start(f32[3,8,32,128]{3,2,1,0:T(8,128)} %source.4) | copy-start | bytes 1179652
  6.2 8.5 %collective-permute-start.4 = (f32[3,4,32,128]{3,2,1,0:T(8,128)S(1)}, f32[3,4,32,128]{3,2,1,0:T(8,128)S(1)}, u32[]{:S(2)}, u32[]{:S(2)}) collective-permute-start(f32[3,4,32,128]{3,2,1,0:T(8,128)S(1)} %get-tuple-element.39), channel_id=1, source_target_pairs={{0,32},{32,64},{64,96},{96,0},{1,33},{33,65},{65,97},{97,1},{2,34}... | collective-permute-start | bytes 589832 | tf_op jit(solution)/shard_map/ppermute | solution.py:455
  6.4 11.0 %collective-permute-start.5 = (f32[3,4,32,128]{3,2,1,0:T(8,128)S(1)}, f32[3,4,32,128]{3,2,1,0:T(8,128)S(1)}, u32[]{:S(2)}, u32[]{:S(2)}) collective-permute-start(f32[3,4,32,128]{3,2,1,0:T(8,128)S(1)} %get-tuple-element.40), channel_id=1, source_target_pairs={{32,0},{64,32},{96,64},{0,96},{33,1},{65,33},{97,65},{1,97},{34,2}... | collective-permute-start | bytes 589832 | tf_op jit(solution)/shard_map/ppermute | solution.py:455
  8.9 1.0 %copy-start.2 = (f32[3,8,32,128]{3,2,1,0:T(8,128)S(1)}, f32[3,8,32,128]{3,2,1,0:T(8,128)}, u32[]{:S(2)}) copy-start(f32[3,8,32,128]{3,2,1,0:T(8,128)} %source.5) | copy-start | bytes 1179652
  10.0 7.4 %collective-permute-start.2 = (f32[3,4,32,128]{3,2,1,0:T(8,128)S(1)}, f32[3,4,32,128]{3,2,1,0:T(8,128)S(1)}, u32[]{:S(2)}, u32[]{:S(2)}) collective-permute-start(f32[3,4,32,128]{3,2,1,0:T(8,128)S(1)} %get-tuple-element.37), channel_id=1, source_target_pairs={{0,32},{32,64},{64,96},{96,0},{1,33},{33,65},{65,97},{97,1},{2,34}... | collective-permute-start | bytes 589832 | tf_op jit(solution)/shard_map/ppermute | solution.py:455
  10.1 7.6 %collective-permute-start.3 = (f32[3,4,32,128]{3,2,1,0:T(8,128)S(1)}, f32[3,4,32,128]{3,2,1,0:T(8,128)S(1)}, u32[]{:S(2)}, u32[]{:S(2)}) collective-permute-start(f32[3,4,32,128]{3,2,1,0:T(8,128)S(1)} %get-tuple-element.38), channel_id=1, source_target_pairs={{32,0},{64,32},{96,64},{0,96},{33,1},{65,33},{97,65},{1,97},{34,2}... | collective-permute-start | bytes 589832 | tf_op jit(solution)/shard_map/ppermute | solution.py:455
  12.8 12.0 %collective-permute-start.6 = (f32[9,4,8,128]{3,2,1,0:T(8,128)S(1)}, f32[9,4,8,128]{3,2,1,0:T(8,128)S(1)}, u32[]{:S(2)}, u32[]{:S(2)}) collective-permute-start(f32[9,4,8,128]{3,2,1,0:T(8,128)S(1)} %get-tuple-element.43), channel_id=1, source_target_pairs={{0,8},{8,16},{16,24},{24,0},{1,9},{9,17},{17,25},{25,1},{2,10},{10... | collective-permute-start | bytes 442376 | tf_op jit(solution)/shard_map/ppermute | solution.py:455
  14.7 10.2 %collective-permute-start.7 = (f32[9,4,8,128]{3,2,1,0:T(8,128)S(1)}, f32[9,4,8,128]{3,2,1,0:T(8,128)S(1)}, u32[]{:S(2)}, u32[]{:S(2)}) collective-permute-start(f32[9,4,8,128]{3,2,1,0:T(8,128)S(1)} %get-tuple-element.44), channel_id=1, source_target_pairs={{8,0},{16,8},{24,16},{0,24},{9,1},{17,9},{25,17},{1,25},{10,2},{18... | collective-permute-start | bytes 442376 | tf_op jit(solution)/shard_map/ppermute | solution.py:455
  17.8 7.1 %collective-permute-start.8 = (f32[9,4,8,128]{3,2,1,0:T(8,128)S(1)}, f32[9,4,8,128]{3,2,1,0:T(8,128)S(1)}, u32[]{:S(2)}, u32[]{:S(2)}) collective-permute-start(f32[9,4,8,128]{3,2,1,0:T(8,128)S(1)} %get-tuple-element.45), channel_id=1, source_target_pairs={{0,8},{8,16},{16,24},{24,0},{1,9},{9,17},{17,25},{25,1},{2,10},{10... | collective-permute-start | bytes 442376 | tf_op jit(solution)/shard_map/ppermute | solution.py:455
  19.5 5.4 %collective-permute-start.9 = (f32[9,4,8,128]{3,2,1,0:T(8,128)S(1)}, f32[9,4,8,128]{3,2,1,0:T(8,128)S(1)}, u32[]{:S(2)}, u32[]{:S(2)}) collective-permute-start(f32[9,4,8,128]{3,2,1,0:T(8,128)S(1)} %get-tuple-element.46), channel_id=1, source_target_pairs={{8,0},{16,8},{24,16},{0,24},{9,1},{17,9},{25,17},{1,25},{10,2},{18... | collective-permute-start | bytes 442376 | tf_op jit(solution)/shard_map/ppermute | solution.py:455
  27.1 5.0 %collective-permute-start.10 = (f32[5,40,128]{2,1,0:T(8,128)S(1)}, f32[5,40,128]{2,1,0:T(8,128)S(1)}, u32[]{:S(2)}, u32[]{:S(2)}) collective-permute-start(f32[5,40,128]{2,1,0:T(8,128)S(1)} %get-tuple-element.57), channel_id=1, source_target_pairs={{0,1},{1,2},{2,3},{3,4},{4,5},{5,6},{6,7},{7,0},{8,9},{9,10},{10,1... | collective-permute-start | bytes 307208 | tf_op jit(solution)/shard_map/ppermute | solution.py:455
  30.3 4.1 %collective-permute-start.11 = (f32[5,40,128]{2,1,0:T(8,128)S(1)}, f32[5,40,128]{2,1,0:T(8,128)S(1)}, u32[]{:S(2)}, u32[]{:S(2)}) collective-permute-start(f32[5,40,128]{2,1,0:T(8,128)S(1)} %get-tuple-element.58), channel_id=1, source_target_pairs={{1,0},{2,1},{3,2},{4,3},{5,4},{6,5},{7,6},{0,7},{9,8},{10,9},{11,1... | collective-permute-start | bytes 307208 | tf_op jit(solution)/shard_map/ppermute | solution.py:455
